TPU v7x, 512 devices: a whole 4x8x8 slice. The times are simulated.
512 devices in a mesh: cells: 128 (over y, x, z_lo, core), obs: 4 (over z_hi).
Axes of the slice: x: 4, y: 8, z: 8 (z_hi: 4, z_lo: 2; z = z_hi * 2 + z_lo), core: 2. Of those that a mesh axis runs over, the one named last changes fastest.
Arguments:
- histories: bfloat16 [64, 384], P('obs'), may hold values from -6 to 6
- amplitude: bfloat16 [64, 5, 131072], P('obs', None, 'cells'), may hold values from -0.75 to 0.75
- weights: bfloat16 [131072, 256], P('cells'), may hold values from -0.375 to 0.375
- retarded: int32 [64, 1024], P('obs', 'cells'), may hold values from 0 to 128
- owner_block: int32 [131072], P('cells'), may hold values from 0 to 127, as said below
- owner_cell: int32 [131072], P('cells'), may hold values from 0 to 16383
- adjoint: float32 [5, 256, 64, 128], P(None, 'cells', 'obs'), may hold values from -6 to 6
- step_size: float32 [256, 64, 128], P('cells', 'obs'), may hold values from 0.1 to 0.6
- jacobian: float32 [128, 3, 5, 5], P('cells'), may hold values from -6 to 6
Outputs:
- adjoint_next: float32 [5, 256, 64, 128], P(None, 'cells', 'obs')
- panel_source: float32 [5, 131072], P(None, 'cells')
Inputs may be any that keep to these rules, and one draw needn't show every extreme that they name: `owner_block`: among each device's 1024 panels at most 32 name one owner block; one owner block, drawn from the seed, is named by exactly 32 panels of every device.
All inputs are finite; a program needn't handle non-finite values.
Results may differ from a plain program's by a relative error of at most 0.0003.
Values sent between devices are 32-bit elements; how exact they have to be, the bound alone decides.
No kernel may reach another device: no remote copies, remote signals or barrier semaphores. Data moves between devices by JAX's collectives and lax.ppermute only.
A program may use at most 192 MiB of HBM per device.

v0:
```python
import jax
import jax.numpy as jnp
from jax import lax
from jax.sharding import PartitionSpec as P

SAMPLES = 256
SPAN = 128
COMP = 5
TILE = 128


smoothing = 0.25


def gathered_total(array, axis):
    blocks = lax.all_gather(array, axis)
    return blocks.sum(axis=0)


def extended(cells, sides, width, closed):
    for axis, dim in sides:
        count = lax.axis_size(axis)
        ends = count if closed else count - 1
        head = lax.slice_in_dim(cells, 0, width, axis=dim)
        tail = lax.slice_in_dim(cells, cells.shape[dim] - width, cells.shape[dim], axis=dim)
        cells = jnp.concatenate(
            [
                lax.ppermute(tail, axis, [(i, (i + 1) % count) for i in range(ends)]),
                cells,
                lax.ppermute(head, axis, [((i + 1) % count, i) for i in range(ends)]),
            ],
            axis=dim,
        )
    return cells


def on_device(
    histories, amplitude, weights, retarded, owner_block, owner_cell, adjoint, step_size, jacobian
):
    tile_count = weights.shape[0] // TILE
    weights_tiled = weights.reshape(tile_count, TILE, SAMPLES)
    observers_local = histories.shape[0]
    history_len = histories.shape[1]
    shifted = jnp.broadcast_to(histories[:, None, :], (observers_local, tile_count, history_len))
    for bit_number in range(SPAN.bit_length()):
        amount = 1 << bit_number
        moved = jnp.concatenate(
            [
                shifted[..., amount:],
                jnp.zeros((observers_local, tile_count, amount), shifted.dtype),
            ],
            axis=2,
        )
        chosen = retarded >> bit_number & 1 == 1
        shifted = jnp.where(chosen[:, :, None], moved, shifted)
    window = shifted[..., :SAMPLES]
    projected = jnp.einsum(
        "tps,ots->otp", weights_tiled, window, preferred_element_type=jnp.float32
    )
    projected = projected.reshape(projected.shape[0], -1)
    partial_value = jnp.sum(amplitude.astype(jnp.float32) * projected[:, None, :], axis=0)
    panel_source = gathered_total(partial_value, "obs")
    my_block = lax.axis_index("cells")
    my_group = lax.axis_index("obs")
    azimuth_local = adjoint.shape[1]
    radial_local = adjoint.shape[2]
    axial_len = adjoint.shape[3]
    radial_all = radial_local * lax.axis_size("obs")
    block_cells = azimuth_local * radial_all * axial_len
    device_cells = azimuth_local * radial_local * axial_len
    target = (owner_block * block_cells + owner_cell).reshape(1, -1)
    empty_field = jnp.zeros((COMP, device_cells), jnp.float32)
    devices = lax.axis_size("cells")
    capacity = 4 * owner_block.shape[0] // devices
    one_hot = (owner_block[:, None] == jnp.arange(devices, dtype=jnp.int32)[None, :]).astype(
        jnp.int32
    )
    slot_rank = jnp.sum(jnp.cumsum(one_hot, axis=0) * one_hot, axis=1) - 1
    slot_of = owner_block * capacity + slot_rank
    outgoing = jnp.zeros((COMP, devices * capacity), jnp.float32).at[:, slot_of].set(panel_source)
    out_index = jnp.full((1, devices * capacity), -1, jnp.int32).at[0, slot_of].set(target[0])
    received, arrivals = (
        lax.all_to_all(outgoing, "cells", split_axis=1, concat_axis=1, tiled=True),
        lax.all_to_all(out_index, "cells", split_axis=1, concat_axis=1, tiled=True),
    )
    flat_index = arrivals[0]
    block_of = flat_index // block_cells
    within = flat_index % block_cells
    azimuth = within // (radial_all * axial_len)
    radius = within // axial_len % radial_all
    axial = within % axial_len
    is_mine = (block_of == my_block) & (radius // radial_local == my_group) & (flat_index >= 0)
    position = (azimuth * radial_local + radius - my_group * radial_local) * axial_len + axial
    landing = jnp.where(is_mine, position, device_cells)
    surface = empty_field.at[:, landing].add(received, mode="drop")
    widened = extended(adjoint, (("cells", 1),), 1, True)
    heightened = extended(adjoint, (("obs", 2),), 1, False)
    deepened = jnp.pad(adjoint, ((0, 0), (0, 0), (0, 0), (1, 1)))
    matrices = jacobian[0]
    neighbours = (
        (widened[:, 2:], widened[:, :-2]),
        (heightened[:, :, 2:], heightened[:, :, :-2]),
        (deepened[..., 2:], deepened[..., :-2]),
    )
    summed = jnp.zeros_like(adjoint)
    for direction in range(3):
        forward, backward = neighbours[direction]
        rotated = jnp.einsum(
            "kc,karz->carz",
            matrices[direction],
            forward - backward,
            precision=lax.Precision.HIGHEST,
        )
        summed = summed + (0.5 * rotated + smoothing * (forward - 2.0 * adjoint + backward))
    adjoint_next = adjoint + step_size[None] * summed + surface.reshape(adjoint.shape)
    return (adjoint_next, panel_source)


def solution(mesh):
    return jax.shard_map(
        on_device,
        mesh=mesh,
        in_specs=(
            P("obs", None),
            P("obs", None, "cells"),
            P("cells", None),
            P("obs", "cells"),
            P("cells"),
            P("cells"),
            P(None, "cells", "obs", None),
            P("cells", "obs", None),
            P("cells", None, None, None),
        ),
        out_specs=(P(None, "cells", "obs", None), P(None, "cells")),
        check_vma=False,
    )
```

profile of v0, /device:TPU:1, one launch (start us, length us, event | category | flops | bytes accessed | tf_op | source)
XLA Modules:
  0.0 114.0 jit_solution(14773806298281911310)
XLA Ops:
  0.7 0.9 copy.97
  1.6 0.2 fusion.16
  1.9 0.1 copy.98
  2.0 0.4 fusion.15
  2.5 0.1 and_reduce_fusion
  2.6 4.3 %scatter_custom_fusion.2 = s32[4096]{0:T(1024)S(1)} fusion(s32[1024]{0:T(1024)S(1)} %broadcast_select_fusion, s32[1024]{0:T(1024)S(1)} %get-tuple-element.25, s32[]{:T(128)} %constant.116.clone.1), kind=kCustom, calls=%fused_computation.79 | custom fusion | bytes 16388
  7.0 0.7 all_to_all.14
  7.7 14.2 %all-to-all-start = ((s32[1,128,32]{2,0,1:T(1,128)}), s32[1,128,32]{2,0,1:T(1,128)S(1)}, u32[]{:S(2)}, u32[]{:S(2)}) async-start(s32[1,128,32]{2,0,1:T(1,128)} %bitcast.14), calls=%async_computation | async-start | bytes 131072 | tf_op jit(solution)/shard_map/all_to_all | solution.py:84
  22.0 1.3 %collective-permute-start.2 = (f32[5,2,1,128]{3,0,2,1:T(8,128)S(1)}, f32[5,2,1,128]{3,0,2,1:T(8,128)S(1)}, u32[]{:S(2)}, u32[]{:S(2)}) collective-permute-start(f32[5,2,1,128]{3,0,2,1:T(8,128)S(1)} %get-tuple-element.13), channel_id=1, source_target_pairs={{1,0},{2,1},{3,2},{5,4},{6,5},{7,6},{9,8},{10,9},{11,10},{13,12},{... | collective-permute-start | bytes 15368 | tf_op jit(solution)/shard_map/ppermute | solution.py:30
  23.3 6.4 %collective-permute-start.3 = (f32[5,2,1,128]{3,0,2,1:T(8,128)S(1)}, f32[5,2,1,128]{3,0,2,1:T(8,128)S(1)}, u32[]{:S(2)}, u32[]{:S(2)}) collective-permute-start(f32[5,2,1,128]{3,0,2,1:T(8,128)S(1)} %get-tuple-element.12), channel_id=1, source_target_pairs={{0,1},{1,2},{2,3},{4,5},{5,6},{6,7},{8,9},{9,10},{10,11},{12,13},{... | collective-permute-start | bytes 15368 | tf_op jit(solution)/shard_map/ppermute | solution.py:28
  29.7 0.7 fusion.33
  30.4 3.1 %collective-permute-start = (f32[5,1,16,128]{3,0,2,1:T(8,128)}, f32[5,1,16,128]{3,0,2,1:T(8,128)S(1)}, u32[]{:S(2)}, u32[]{:S(2)}) collective-permute-start(f32[5,1,16,128]{3,0,2,1:T(8,128)} %get-tuple-element.11), channel_id=1, source_target_pairs={{4,0},{8,4},{12,8},{16,12},{20,16},{24,20},{28,24},{32,28},{36,32}... | collective-permute-start | bytes 122888 | tf_op jit(solution)/shard_map/ppermute | solution.py:30
  33.5 2.7 %collective-permute-start.1 = (f32[5,1,16,128]{3,0,2,1:T(8,128)}, f32[5,1,16,128]{3,0,2,1:T(8,128)S(1)}, u32[]{:S(2)}, u32[]{:S(2)}) collective-permute-start(f32[5,1,16,128]{3,0,2,1:T(8,128)} %get-tuple-element.10), channel_id=1, source_target_pairs={{0,4},{4,8},{8,12},{12,16},{16,20},{20,24},{24,28},{28,32},{32,36}... | collective-permute-start | bytes 122888 | tf_op jit(solution)/shard_map/ppermute | solution.py:28
  36.4 0.1 slice.110
  36.5 0.1 pad_select_fusion.5
  36.6 0.1 slice.111
  36.7 0.1 pad_select_fusion.4
  36.8 0.1 slice.112
  36.9 0.1 pad_select_fusion.3
  37.0 0.1 slice.113
  37.1 0.1 pad_select_fusion.2
  37.2 0.1 slice.114
  37.3 0.1 pad_select_fusion.1
  37.4 0.1 slice.115
  37.5 0.1 pad_select_fusion
  37.6 0.3 convolution_bitcast_fusion
  38.0 1.1 fusion.10
  39.1 14.6 %all-gather.1 = f32[4,5,1024]{2,1,0:T(8,128)S(1)} all-gather(f32[1,5,1024]{2,1,0:T(8,128)S(1)} %bitcast.73), channel_id=2, replica_groups=mesh['cells'=128,'obs'=4] {'obs'}, dimensions={0}, use_global_device_ids=true | all-gather | bytes 102400 | tf_op jit(solution)/shard_map/all_gather | solution.py:16
  53.7 0.2 copy.101
  53.9 3.6 %scatter_custom_fusion = f32[5,4096]{0,1:T(8,128)S(1)} fusion(s32[1024]{0:T(1024)S(1)} %get-tuple-element.26, f32[1024,5]{1,0:T(8,128)S(1)} %copy.101, f32[]{:T(128)} %constant.115.clone.1), kind=kCustom, calls=%fused_computation.20 | custom fusion | bytes 81924 | tf_op jit(solution)/shard_map/scatter | solution.py:80
  57.5 0.8 copy.102
  58.4 0.9 reshape.416
  59.3 0.3 fusion.9
  59.6 14.3 %all-to-all-start.1 = ((f32[128,1,160]{2,1,0:T(1,128)}), f32[128,1,160]{2,1,0:T(1,128)S(1)}, u32[]{:S(2)}, u32[]{:S(2)}) async-start(f32[128,1,160]{2,1,0:T(1,128)} %reshape.416), calls=%async_computation.1 | async-start | bytes 262144 | tf_op jit(solution)/shard_map/all_to_all | solution.py:83
  73.9 0.5 broadcast.466
  74.4 0.8 reduce.8
  75.3 0.1 squeeze.16
  75.4 0.5 compare_select_fusion
  75.8 9.5 %all-to-all-done.1 = f32[128,1,160]{2,1,0:T(1,128)S(1)} async-done(((f32[128,1,160]{2,1,0:T(1,128)}), f32[128,1,160]{2,1,0:T(1,128)S(1)}, u32[]{:S(2)}, u32[]{:S(2)}) %all-to-all-start.1) | async-done | bytes 81952 | tf_op jit(solution)/shard_map/all_to_all | solution.py:83
  85.4 0.5 broadcast.467
  85.9 1.0 reduce.9
  86.8 0.1 reshape.417
  87.0 0.2 reshape.380
  87.2 2.0 %copy.104 = f32[4096,5]{1,0:T(8,128)} copy(f32[4096,5]{0,1:T(8,128)S(1)} %bitcast.70) | data formatting | bytes 163840 | tf_op jit(solution)/shard_map/all_to_all | solution.py:83
  89.2 23.2 %scatter_custom_fusion.1 = f32[5,4096]{0,1:T(8,128)S(1)} fusion(s32[4096]{0:T(1024)S(1)} %bitcast.77, f32[4096,5]{1,0:T(8,128)} %copy.104, f32[]{:T(128)} %constant.115.clone.1), kind=kCustom, calls=%fused_computation.18 | custom fusion | flops 20480 | bytes 82432 | tf_op jit(solution)/shard_map/scatter-add | solution.py:95
  112.4 0.6 copy.106
  113.0 0.3 fusion.8
  113.4 0.7 copy.107
  (50 shorter events, 0.7 us)
Async XLA Ops:
  0.6 37.0 %copy-start = (bf16[1024,256]{1,0:T(8,128)(2,1)S(1)}, bf16[1024,256]{1,0:T(8,128)(2,1)}, u32[]{:S(2)}) copy-start(bf16[1024,256]{1,0:T(8,128)(2,1)} %param.11) | copy-start | bytes 1572868
  0.6 1.8 %copy-start.11 = (s32[2]{0:T(128)S(1)}, s32[2]{0:T(128)}, u32[]{:S(2)}) copy-start(s32[2]{0:T(128)} %constant.166) | copy-start | bytes 28
  0.7 1.9 %copy-start.12 = (s32[2]{0:T(128)S(1)}, s32[2]{0:T(128)}, u32[]{:S(2)}) copy-start(s32[2]{0:T(128)} %constant.169) | copy-start | bytes 28
  0.7 1.4 %copy-start.6 = (s32[1024]{0:T(1024)S(1)}, s32[1024]{0:T(1024)}, u32[]{:S(2)}) copy-start(s32[1024]{0:T(1024)} %param.13) | copy-start | bytes 12292
  0.7 1.7 %copy-start.9 = (s32[1024]{0:T(1024)S(1)}, s32[1024]{0:T(1024)}, u32[]{:S(2)}) copy-start(s32[1024]{0:T(1024)} %param.14) | copy-start | bytes 12292
  0.7 21.2 %copy-start.5 = (f32[5,2,16,128]{3,2,1,0:T(8,128)S(1)}, f32[5,2,16,128]{3,2,1,0:T(8,128)}, u32[]{:S(2)}) copy-start(f32[5,2,16,128]{3,2,1,0:T(8,128)} %param.15) | copy-start | bytes 245764
  0.7 35.4 %copy-start.10 = (s32[16,8]{0,1:T(8,128)S(1)}, s32[16,8]{0,1:T(8,128)}, u32[]{:S(2)}) copy-start(s32[16,8]{0,1:T(8,128)} %param.12) | copy-start | bytes 1540
  0.7 35.4 %copy-start.1 = (bf16[16,384]{1,0:T(8,128)(2,1)S(1)}, bf16[16,384]{1,0:T(8,128)(2,1)}, u32[]{:S(2)}) copy-start(bf16[16,384]{1,0:T(8,128)(2,1)} %param.9) | copy-start | bytes 36868
  7.7 51.9 %all-to-all-start = ((s32[1,128,32]{2,0,1:T(1,128)}), s32[1,128,32]{2,0,1:T(1,128)S(1)}, u32[]{:S(2)}, u32[]{:S(2)}) async-start(s32[1,128,32]{2,0,1:T(1,128)} %bitcast.14), calls=%async_computation | async-start | bytes 131072 | tf_op jit(solution)/shard_map/all_to_all | solution.py:84
  22.0 37.3 %collective-permute-start.2 = (f32[5,2,1,128]{3,0,2,1:T(8,128)S(1)}, f32[5,2,1,128]{3,0,2,1:T(8,128)S(1)}, u32[]{:S(2)}, u32[]{:S(2)}) collective-permute-start(f32[5,2,1,128]{3,0,2,1:T(8,128)S(1)} %get-tuple-element.13), channel_id=1, source_target_pairs={{1,0},{2,1},{3,2},{5,4},{6,5},{7,6},{9,8},{10,9},{11,10},{13,12},{... | collective-permute-start | bytes 15368 | tf_op jit(solution)/shard_map/ppermute | solution.py:30
  23.3 36.0 %collective-permute-start.3 = (f32[5,2,1,128]{3,0,2,1:T(8,128)S(1)}, f32[5,2,1,128]{3,0,2,1:T(8,128)S(1)}, u32[]{:S(2)}, u32[]{:S(2)}) collective-permute-start(f32[5,2,1,128]{3,0,2,1:T(8,128)S(1)} %get-tuple-element.12), channel_id=1, source_target_pairs={{0,1},{1,2},{2,3},{4,5},{5,6},{6,7},{8,9},{9,10},{10,11},{12,13},{... | collective-permute-start | bytes 15368 | tf_op jit(solution)/shard_map/ppermute | solution.py:28
  30.4 82.6 %collective-permute-start = (f32[5,1,16,128]{3,0,2,1:T(8,128)}, f32[5,1,16,128]{3,0,2,1:T(8,128)S(1)}, u32[]{:S(2)}, u32[]{:S(2)}) collective-permute-start(f32[5,1,16,128]{3,0,2,1:T(8,128)} %get-tuple-element.11), channel_id=1, source_target_pairs={{4,0},{8,4},{12,8},{16,12},{20,16},{24,20},{28,24},{32,28},{36,32}... | collective-permute-start | bytes 122888 | tf_op jit(solution)/shard_map/ppermute | solution.py:30
  33.5 79.6 %collective-permute-start.1 = (f32[5,1,16,128]{3,0,2,1:T(8,128)}, f32[5,1,16,128]{3,0,2,1:T(8,128)S(1)}, u32[]{:S(2)}, u32[]{:S(2)}) collective-permute-start(f32[5,1,16,128]{3,0,2,1:T(8,128)} %get-tuple-element.10), channel_id=1, source_target_pairs={{0,4},{4,8},{8,12},{12,16},{16,20},{20,24},{24,28},{28,32},{32,36}... | collective-permute-start | bytes 122888 | tf_op jit(solution)/shard_map/ppermute | solution.py:28
  36.2 1.7 %copy-start.8 = (f32[1,3,5,5]{3,0,2,1:T(1,128)S(1)}, f32[1,3,5,5]{3,0,2,1:T(1,128)}, u32[]{:S(2)}) copy-start(f32[1,3,5,5]{3,0,2,1:T(1,128)} %param.17) | copy-start | bytes 904
  36.5 2.6 %copy-start.2 = (bf16[16,5,1024]{2,0,1:T(8,128)(2,1)S(1)}, bf16[16,5,1024]{2,0,1:T(8,128)(2,1)}, u32[]{:S(2)}) copy-start(bf16[16,5,1024]{2,0,1:T(8,128)(2,1)} %param.10) | copy-start | bytes 491524
  53.7 4.7 %copy-start.3 = (f32[5,1024]{1,0:T(8,128)}, f32[5,1024]{1,0:T(8,128)S(1)}, u32[]{:S(2)}) copy-start(f32[5,1024]{1,0:T(8,128)S(1)} %reduce_sum.29) | copy-start | bytes 61444
  59.6 25.8 %all-to-all-start.1 = ((f32[128,1,160]{2,1,0:T(1,128)}), f32[128,1,160]{2,1,0:T(1,128)S(1)}, u32[]{:S(2)}, u32[]{:S(2)}) async-start(f32[128,1,160]{2,1,0:T(1,128)} %reshape.416), calls=%async_computation.1 | async-start | bytes 262144 | tf_op jit(solution)/shard_map/all_to_all | solution.py:83
  89.2 23.8 %copy-start.4 = (f32[5,2,16,128]{3,0,2,1:T(8,128)S(1)}, f32[5,2,16,128]{3,0,2,1:T(8,128)}, u32[]{:S(2)}) copy-start(f32[5,2,16,128]{3,0,2,1:T(8,128)} %fusion.10) | copy-start | bytes 245764
  89.2 23.8 %copy-start.7 = (f32[2,16,128]{2,1,0:T(8,128)S(1)}, f32[2,16,128]{2,1,0:T(8,128)}, u32[]{:S(2)}) copy-start(f32[2,16,128]{2,1,0:T(8,128)} %param.16) | copy-start | bytes 49156
where the time goes:
time: 114 us
  starting transfers between devices  42 us (37%)
  other arithmetic  27 us (24%)
  local copies, waits for them, and re-layouts  17.8 us (16%)
  blocking collectives  14.6 us (13%)
  waiting for transfers between devices  9.56 us (8%)
  matrix products  2.01 us (2%)
  between operations  1.16 us (1%)
    scatter-add x1, other arithmetic, on_device(): surface = empty_field.at[:, landing].add(received, mode='drop')  23.2 us
    all_gather x1, blocking collectives, gathered_total(): blocks = lax.all_gather(array, axis)  14.6 us
    all_to_all x1, starting transfers between devices, on_device(): lax.all_to_all(outgoing, 'cells', split_axis=1, concat_axis=1, tiled=True)  14.3 us
    all_to_all x1, starting transfers between devices, on_device(): lax.all_to_all(out_index, 'cells', split_axis=1, concat_axis=1, tiled=True)  14.2 us
    all_to_all x1, waiting for transfers between devices, on_device(): lax.all_to_all(outgoing, 'cells', split_axis=1, concat_axis=1, tiled=True)  9.54 us
    ppermute x2, starting transfers between devices, extended(): lax.ppermute(tail, axis, [(i, (i + 1) % count) for i in range(ends)])  9.09 us
    unnamed x31, local copies, waits for them, and re-layouts  6.15 us
    ppermute x2, starting transfers between devices, extended(): lax.ppermute(head, axis, [((i + 1) % count, i) for i in range(ends)])  4.36 us
  transfers between devices with their start and end apart: 6, of which 1 were waited for; matrix products, arithmetic and copies ran while one was open for 34% of the time, Pallas kernels for 0%

commit v1 on v0

v1 whole, which is shorter than its diff:
```python
import jax
import jax.numpy as jnp
from jax import lax
from jax.experimental import pallas as pl
from jax.experimental.pallas import tpu as pltpu
from jax.sharding import PartitionSpec as P

TILE = 128
COMP = 5
CAP = 32
SMOOTHING = 0.25
F32 = jnp.float32
BF16 = jnp.bfloat16
NT = (((1,), (1,)), ((), ()))

VMEM = pl.BlockSpec(memory_space=pltpu.MemorySpace.VMEM)
SMEM = pl.BlockSpec(memory_space=pltpu.MemorySpace.SMEM)
ANY = pl.BlockSpec(memory_space=pl.ANY)


def iota(shape, dim):
    return lax.broadcasted_iota(jnp.int32, shape, dim)


def split(x):
    high = x.astype(BF16)
    return high, (x - high.astype(F32)).astype(BF16)


def project(hist_ref, amp_ref, weight_ref, ret_ref, adj_ref, out_ref):
    observers = hist_ref.shape[0]
    tiles = ret_ref.shape[1]
    hist = hist_ref[...].astype(F32)
    rows = tiles * observers
    column = [jnp.concatenate([hist[:, j * 128 : (j + 1) * 128]] * tiles, axis=0) for j in range(3)]
    shift = jnp.concatenate(
        [jnp.broadcast_to(ret_ref[:, t : t + 1], (observers, 128)) for t in range(tiles)], axis=0
    )
    lane = iota((rows, 128), 1)
    far = shift >= 128
    column = [
        jnp.where(far, column[1], column[0]),
        jnp.where(far, column[2], column[1]),
        column[2],
    ]
    for amount in (64, 32, 16, 8, 4, 2, 1):
        turned = [pltpu.roll(x, 128 - amount, 1) for x in column]
        stays = lane < 128 - amount
        chosen = (shift & amount) != 0
        column = [
            jnp.where(chosen, jnp.where(stays, turned[0], turned[1]), column[0]),
            jnp.where(chosen, jnp.where(stays, turned[1], turned[2]), column[1]),
            jnp.where(chosen, turned[2], column[2]),
        ]
    window = jnp.concatenate(column[:2], axis=1).astype(BF16)
    for t in range(tiles):
        span = slice(t * TILE, (t + 1) * TILE)
        projected = lax.dot_general(
            window[t * observers : (t + 1) * observers],
            weight_ref[span, :],
            NT,
            preferred_element_type=F32,
        )
        total = jnp.zeros((COMP, TILE), F32)
        for o in range(observers):
            total = total + amp_ref[o, :, span].astype(F32) * projected[o : o + 1, :]
        for copy in range(out_ref.shape[0]):
            out_ref[copy, :COMP, span] = total
    azimuths, radii = adj_ref.shape[1:3]
    place = 0
    for row in (0, radii - 1):
        for c in range(COMP):
            for a in range(azimuths):
                line = adj_ref[c, a, row : row + 1, :]
                where = (COMP + place // 8, place % 8 * 128)
                for copy in range(out_ref.shape[0]):
                    out_ref[copy, where[0] : where[0] + 1, where[1] : where[1] + 128] = line
                place += 1
    for rest in range(place, 24):
        for copy in range(out_ref.shape[0]):
            out_ref[copy, COMP + rest // 8 : COMP + rest // 8 + 1, rest % 8 * 128 : (rest % 8 + 1) * 128] = jnp.zeros(
                (1, 128), F32
            )


def radial_line(ref, group, side, c, a):
    place = side * 10 + c * 2 + a
    return ref[group, COMP + place // 8, pl.ds(place % 8 * 128, 128)].reshape(1, 128)


def order(after_ref, block_ref, adj_ref, rank_ref, head_ref, tail_ref):
    chunks, width = block_ref.shape
    blocks = 128
    head_ref[...] = adj_ref[:, 0]
    tail_ref[...] = adj_ref[:, adj_ref.shape[1] - 1]
    mark = jnp.where((iota((width, 2 * width), 0) < iota((width, 2 * width), 1)), 1.0, 0.0).astype(BF16)
    before = jnp.zeros((blocks, width), F32)
    for j in range(chunks):
        same = iota((blocks, width), 0) == block_ref[j : j + 1, :]
        counted = jnp.dot(jnp.where(same, 1.0, 0.0).astype(BF16), mark, preferred_element_type=F32)
        rank_ref[j : j + 1, :] = jnp.sum(
            jnp.where(same, counted[:, :width] + before, 0.0), axis=0, keepdims=True
        )
        before = before + counted[:, width:]


def pack(part_ref, block_ref, cell_ref, rank_ref, source_ref, out_ref):
    chunks, width = block_ref.shape
    source = part_ref[0, :COMP, :]
    for group in range(1, part_ref.shape[0]):
        source = source + part_ref[group, :COMP, :]
    source_ref[...] = source
    total = jnp.zeros((128, (COMP + 1) * CAP), F32)
    for j in range(chunks):
        span = slice(j * width, (j + 1) * width)
        slot = iota((CAP, width), 0).astype(F32) == rank_ref[j : j + 1, :]
        same = jnp.where(iota((128, width), 0) == block_ref[j : j + 1, :], 1.0, 0.0).astype(BF16)
        lines = [source[c : c + 1, span] for c in range(COMP)] + [cell_ref[j : j + 1, :].astype(F32)]
        placed = jnp.concatenate([jnp.where(slot, line, 0.0) for line in lines], axis=0)
        high, low = split(placed)
        total = (
            total
            + lax.dot_general(same, high, NT, preferred_element_type=F32)
            + lax.dot_general(same, low, NT, preferred_element_type=F32)
        )
    out_ref[:, :128] = total[:, :128]
    out_ref[:, 128:] = jnp.concatenate([total[:, 128:], jnp.zeros((128, 64), F32)], axis=1)


def stencil(part_ref, next_ref, prev_ref, adj_ref, step_ref, jac_ref, out_ref):
    group = lax.axis_index("obs")
    groups = part_ref.shape[0]
    azimuths, radii, length = adj_ref.shape[1:]
    row = iota((radii, length), 0)
    lane = iota((radii, length), 1)
    below = jnp.maximum(group - 1, 0)
    above = jnp.minimum(group + 1, groups - 1)
    has_below = jnp.where(group > 0, 1.0, 0.0)
    has_above = jnp.where(group < groups - 1, 1.0, 0.0)
    for a in range(azimuths):
        centre = [adj_ref[c, a] for c in range(COMP)]
        pairs = [[], [], []]
        for c in range(COMP):
            x = centre[c]
            ahead = next_ref[c] if a == azimuths - 1 else adj_ref[c, a + 1]
            behind = prev_ref[c] if a == 0 else adj_ref[c, a - 1]
            pairs[0].append((ahead, behind))
            upper = radial_line(part_ref, above, 0, c, a) * has_above
            lower = radial_line(part_ref, below, 1, c, a) * has_below
            pairs[1].append(
                (
                    jnp.where(row == radii - 1, upper, pltpu.roll(x, radii - 1, 0)),
                    jnp.where(row == 0, lower, pltpu.roll(x, 1, 0)),
                )
            )
            pairs[2].append(
                (
                    jnp.where(lane == length - 1, 0.0, pltpu.roll(x, length - 1, 1)),
                    jnp.where(lane == 0, 0.0, pltpu.roll(x, 1, 1)),
                )
            )
        differences = [[f - b for f, b in pairs[d]] for d in range(3)]
        for c in range(COMP):
            rotated = jnp.zeros((radii, length), F32)
            spread = -6.0 * centre[c]
            for d in range(3):
                spread = spread + (pairs[d][c][0] + pairs[d][c][1])
                for k in range(COMP):
                    rotated = rotated + jac_ref[0, d, k, c] * differences[d][k]
            summed = 0.5 * rotated + SMOOTHING * spread
            out_ref[c, a] = centre[c] + step_ref[a] * summed


def land(got_ref, base_ref, out_ref):
    group = lax.axis_index("obs")
    azimuths, radii, length = base_ref.shape[1:]
    radii_all = radii * lax.axis_size("obs")
    local_rows = azimuths * radii
    got = jnp.concatenate([got_ref[:, :128].T, got_ref[:, 128:].T], axis=0)
    sources = got_ref.shape[0]
    high, low = split(got)
    high, low = high.astype(F32), low.astype(F32)
    cell = got[COMP * CAP : (COMP + 1) * CAP].astype(jnp.int32)
    cell_row = cell >> 7
    cell_lane = cell & 127
    local = iota((local_rows, sources), 0)
    wanted = (local // radii) * radii_all + local % radii + group * radii
    total = jnp.zeros((COMP * local_rows, length), F32)
    for first in range(0, CAP, 2):
        highs, lows, lanes = [], [], []
        for k in (first, first + 1):
            here = wanted == cell_row[k : k + 1]
            highs.append(
                jnp.concatenate([jnp.where(here, high[c * CAP + k : c * CAP + k + 1], 0.0) for c in range(COMP)], axis=0).astype(BF16)
            )
            lows.append(
                jnp.concatenate([jnp.where(here, low[c * CAP + k : c * CAP + k + 1], 0.0) for c in range(COMP)], axis=0).astype(BF16)
            )
            lanes.append(jnp.where(iota((length, sources), 0) == cell_lane[k : k + 1], 1.0, 0.0).astype(BF16))
        at = jnp.concatenate(lanes, axis=1)
        total = (
            total
            + lax.dot_general(jnp.concatenate(highs, axis=1), at, NT, preferred_element_type=F32)
            + lax.dot_general(jnp.concatenate(lows, axis=1), at, NT, preferred_element_type=F32)
        )
    for c in range(COMP):
        for a in range(azimuths):
            start = (c * azimuths + a) * radii
            out_ref[c, a] = base_ref[c, a] + total[start : start + radii]


def on_device(
    histories, amplitude, weights, retarded, owner_block, owner_cell, adjoint, step_size, jacobian
):
    groups = lax.axis_size("obs")
    count = lax.axis_size("cells")
    panels = weights.shape[0]
    blocks2 = owner_block.reshape(panels // 128, 128)
    cells2 = owner_cell.reshape(panels // 128, 128)
    shape = jax.ShapeDtypeStruct

    partial_copies = pl.pallas_call(
        project,
        out_shape=shape((groups, 8, panels), F32),
        in_specs=[VMEM] * 5,
        out_specs=VMEM,
        name="project",
    )(histories, amplitude, weights, retarded, adjoint)
    parts = lax.all_to_all(partial_copies, "obs", split_axis=0, concat_axis=0, tiled=True)

    edge = shape((COMP,) + adjoint.shape[2:], F32)
    rank, head, tail = pl.pallas_call(
        order,
        out_shape=(shape(blocks2.shape, F32), edge, edge),
        in_specs=[ANY, VMEM, VMEM],
        out_specs=(VMEM, VMEM, VMEM),
        name="order",
    )(partial_copies, blocks2, adjoint)
    panel_source, outgoing = pl.pallas_call(
        pack,
        out_shape=(shape((COMP, panels), F32), shape((count, 256), F32)),
        in_specs=[VMEM] * 4,
        out_specs=(VMEM, VMEM),
        name="pack",
    )(parts, blocks2, cells2, rank)
    received = lax.all_to_all(outgoing, "cells", split_axis=0, concat_axis=0, tiled=True)

    behind = lax.ppermute(tail, "cells", [(i, (i + 1) % count) for i in range(count)])
    ahead = lax.ppermute(head, "cells", [((i + 1) % count, i) for i in range(count)])
    base = pl.pallas_call(
        stencil,
        out_shape=shape(adjoint.shape, F32),
        in_specs=[VMEM] * 5 + [SMEM],
        out_specs=VMEM,
        name="stencil",
    )(parts, ahead, behind, adjoint, step_size, jacobian)
    adjoint_next = pl.pallas_call(
        land,
        out_shape=shape(adjoint.shape, F32),
        in_specs=[VMEM] * 2,
        out_specs=VMEM,
        name="land",
    )(received, base)
    return adjoint_next, panel_source


def solution(mesh):
    return jax.shard_map(
        on_device,
        mesh=mesh,
        in_specs=(
            P("obs", None),
            P("obs", None, "cells"),
            P("cells", None),
            P("obs", "cells"),
            P("cells"),
            P("cells"),
            P(None, "cells", "obs", None),
            P("cells", "obs", None),
            P("cells", None, None, None),
        ),
        out_specs=(P(None, "cells", "obs", None), P(None, "cells")),
        check_vma=False,
    )
```

time: 114 us -> 62.2 us (0.55)
  the two profiles are of different devices: /device:TPU:1 before, /device:TPU:32 now
where the time goes in v1:
time: 62.2 us; the launch traced here: 61.7 us
  starting transfers between devices  28.9 us (46%)
  waiting for transfers between devices  14.5 us (23%)
  Pallas kernels  11 us (18%)
  local copies, waits for them, and re-layouts  6.6 us (11%)
  between operations  0.7 us (1%)
    all_to_all x1, starting transfers between devices, on_device(): lax.all_to_all(outgoing, 'cells', split_axis=0, concat_axis=0, tiled=True)  11.5 us
    all_to_all x1, starting transfers between devices, on_device(): lax.all_to_all(partial_copies, 'obs', split_axis=0, concat_axis=0, tiled=...  10.3 us
    all_to_all x1, waiting for transfers between devices, on_device(): lax.all_to_all(partial_copies, 'obs', split_axis=0, concat_axis=0, tiled=...  7.49 us
    ppermute x1, waiting for transfers between devices, on_device(): lax.ppermute(tail, 'cells', [(i, (i + 1) % count) for i in range(count)])  7 us
    ppermute x1, starting transfers between devices, on_device(): lax.ppermute(head, 'cells', [((i + 1) % count, i) for i in range(count)])  5.19 us
    unnamed x18, local copies, waits for them, and re-layouts  4.92 us
    pallas_call x1, Pallas kernels, on_device(): pl.pallas_call(project, out_shape=shape((groups, 8, panels), F32), in_spe...  2.68 us
    pallas_call x1, Pallas kernels, on_device(): pl.pallas_call(land, out_shape=shape(adjoint.shape, F32), in_specs=[VMEM]...  2.52 us
  transfers between devices with their start and end apart: 4, of which 2 were waited for; matrix products, arithmetic and copies ran while one was open for 1% of the time, Pallas kernels for 6%

profile of v1, /device:TPU:32, one launch (start us, length us, event | category | flops | bytes accessed | tf_op | source)
XLA Modules:
  0.0 61.7 jit_solution(4527336307258439205)
XLA Ops:
  0.6 0.0 copy-start.4
  0.6 1.7 %copy.14.amp_ref = bf16[16,5,1024]{2,1,0:T(8,128)(2,1)} copy(bf16[16,5,1024]{2,0,1:T(8,128)(2,1)} %param.10) | data formatting | bytes 327680 | tf_op args[1]
  2.4 0.0 copy-done.4
  2.4 0.7 %copy.15.ret_ref = s32[16,8]{1,0:T(8,128)} copy(s32[16,8]{0,1:T(8,128)S(1)} %copy-done.4) | data formatting | bytes 1024 | tf_op args[3]
  3.0 2.7 %project.1.after_ref = f32[4,8,1024]{2,1,0:T(8,128)} custom-call(bf16[16,384]{1,0:T(8,128)(2,1)} %hist_ref.1, bf16[16,5,1024]{2,1,0:T(8,128)(2,1)} %copy.14.amp_ref, bf16[1024,256]{1,0:T(8,128)(2,1)} %weight_ref.1, s32[16,8]{1,0:T(8,128)} %copy.15.ret_ref, f32[5,2,16,128]{3,2,1,0:T(8,128)} %adj_ref.5), custom_call_target="tpu_custom_call" | custom-call | tf_op jit(solution)/shard_map/project/pallas_call | solution.py:222
  5.7 10.3 %all-to-all-start = ((f32[4,8,1024]{2,1,0:T(8,128)}), f32[4,8,1024]{2,1,0:T(8,128)S(1)}, u32[]{:S(2)}, u32[]{:S(2)}) async-start(f32[4,8,1024]{2,1,0:T(8,128)} %project.1.after_ref), calls=%async_computation | async-start | bytes 262144 | tf_op jit(solution)/shard_map/all_to_all | solution.py:229
  16.0 1.8 %order.1 = (f32[8,128]{1,0:T(8,128)}, f32[5,16,128]{2,1,0:T(8,128)}, f32[5,16,128]{2,1,0:T(8,128)}) custom-call(f32[4,8,1024]{2,1,0:T(8,128)} %project.1.after_ref, s32[8,128]{1,0:T(8,128)} %bitcast.8, f32[5,2,16,128]{3,2,1,0:T(8,128)} %adj_ref.5), custom_call_target="tpu_custom_call" | custom-call | tf_op jit(solution)/shard_map/order/pallas_call | solution.py:232
  17.8 7.5 %all-to-all-done.part_ref = f32[4,8,1024]{2,1,0:T(8,128)S(1)} async-done(((f32[4,8,1024]{2,1,0:T(8,128)}), f32[4,8,1024]{2,1,0:T(8,128)S(1)}, u32[]{:S(2)}, u32[]{:S(2)}) %all-to-all-start) | async-done | bytes 131104 | tf_op jit(solution)/shard_map/all_to_all | solution.py:229
  25.3 0.0 copy-start
  25.3 0.6 %copy-done = f32[4,8,1024]{2,1,0:T(8,128)} copy-done((f32[4,8,1024]{2,1,0:T(8,128)}, f32[4,8,1024]{2,1,0:T(8,128)S(1)}, u32[]{:S(2)}) %copy-start) | copy-done | bytes 131096
  25.9 2.2 %pack.1 = (f32[5,1024]{1,0:T(8,128)}, f32[128,256]{1,0:T(8,128)}) custom-call(f32[4,8,1024]{2,1,0:T(8,128)} %copy-done, s32[8,128]{1,0:T(8,128)} %bitcast.9, s32[8,128]{1,0:T(8,128)} %bitcast.10, f32[8,128]{1,0:T(8,128)} %get-tuple-element.7.rank_ref), custom_call_target="tpu_custom_call" | custom-call | tf_op jit(solution)/shard_map/pack/pallas_call | solution.py:239
  28.2 1.7 %copy.16 = f32[128,1,256]{2,1,0:T(1,128)} copy(f32[128,1,256]{2,0,1:T(8,128)} %bitcast.7) | data formatting | bytes 262144 | tf_op jit(solution)/shard_map/all_to_all | solution.py:246
  29.8 0.0 copy-start.6
  29.8 0.0 copy-start.5
  29.9 0.0 copy-start.3
  29.9 11.5 %all-to-all-start.1 = ((f32[128,1,256]{2,1,0:T(1,128)}), f32[128,1,256]{2,1,0:T(1,128)S(1)}, u32[]{:S(2)}, u32[]{:S(2)}) async-start(f32[128,1,256]{2,1,0:T(1,128)} %copy.16), calls=%async_computation.1 | async-start | bytes 262144 | tf_op jit(solution)/shard_map/all_to_all | solution.py:246
  41.3 0.0 copy-done.6
  41.3 5.2 %collective-permute-start = (f32[5,16,128]{2,1,0:T(8,128)S(1)}, f32[5,16,128]{2,1,0:T(8,128)S(1)}, u32[]{:S(2)}, u32[]{:S(2)}) collective-permute-start(f32[5,16,128]{2,1,0:T(8,128)S(1)} %copy-done.6), channel_id=1, source_target_pairs={{4,0},{8,4},{12,8},{16,12},{20,16},{24,20},{28,24},{32,28},{36,32}... | collective-permute-start | bytes 122888 | tf_op jit(solution)/shard_map/ppermute | solution.py:249
  46.5 0.0 copy-done.5
  46.5 1.9 %collective-permute-start.1 = (f32[5,16,128]{2,1,0:T(8,128)S(1)}, f32[5,16,128]{2,1,0:T(8,128)S(1)}, u32[]{:S(2)}, u32[]{:S(2)}) collective-permute-start(f32[5,16,128]{2,1,0:T(8,128)S(1)} %copy-done.5), channel_id=1, source_target_pairs={{0,4},{4,8},{8,12},{12,16},{16,20},{20,24},{24,28},{28,32},{32,36}... | collective-permute-start | bytes 122888 | tf_op jit(solution)/shard_map/ppermute | solution.py:248
  48.5 0.0 copy-done.3
  48.5 0.6 copy.17.jac_ref
  49.1 0.0 collective-permute-done.next_ref
  49.1 0.0 copy-start.1
  49.1 7.0 %collective-permute-done.1.prev_ref = f32[5,16,128]{2,1,0:T(8,128)S(1)} collective-permute-done((f32[5,16,128]{2,1,0:T(8,128)S(1)}, f32[5,16,128]{2,1,0:T(8,128)S(1)}, u32[]{:S(2)}, u32[]{:S(2)}) %collective-permute-start.1) | collective-permute-done | bytes 40992 | tf_op jit(solution)/shard_map/ppermute | solution.py:248
  56.1 0.0 copy-done.1
  56.1 0.0 copy-start.2
  56.1 0.6 copy-done.2
  56.7 1.8 %stencil.1.base_ref = f32[5,2,16,128]{3,2,1,0:T(8,128)} custom-call(f32[4,8,1024]{2,1,0:T(8,128)} %copy-done, f32[5,16,128]{2,1,0:T(8,128)} %copy-done.1, f32[5,16,128]{2,1,0:T(8,128)} %copy-done.2, f32[5,2,16,128]{3,2,1,0:T(8,128)} %adj_ref.5, f32[2,16,128]{2,1,0:T(8,128)} %step_ref.1, f32[1,3,5,5]{3,2,1,0:T(8,128)} %copy.17.jac_ref), custom_call_target="tpu_custom_call" | custom-call | tf_op jit(solution)/shard_map/stencil/pallas_call | solution.py:250
  58.5 0.0 all-to-all-done.1
  58.5 0.7 %copy.20 = f32[128,1,256]{2,0,1:T(8,128)} copy(f32[128,1,256]{2,1,0:T(1,128)S(1)} %all-to-all-done.1) | data formatting | bytes 262144
  59.1 2.5 %land.1 = f32[5,2,16,128]{3,2,1,0:T(8,128)} custom-call(f32[128,256]{1,0:T(8,128)} %bitcast.6, f32[5,2,16,128]{3,2,1,0:T(8,128)} %stencil.1.base_ref), custom_call_target="tpu_custom_call" | custom-call | tf_op jit(solution)/shard_map/land/pallas_call | solution.py:257
Async XLA Ops:
  0.6 1.7 %copy-start.4 = (s32[16,8]{0,1:T(8,128)S(1)}, s32[16,8]{0,1:T(8,128)}, u32[]{:S(2)}) copy-start(s32[16,8]{0,1:T(8,128)} %param.12) | copy-start | bytes 1540
  5.7 19.6 %all-to-all-start = ((f32[4,8,1024]{2,1,0:T(8,128)}), f32[4,8,1024]{2,1,0:T(8,128)S(1)}, u32[]{:S(2)}, u32[]{:S(2)}) async-start(f32[4,8,1024]{2,1,0:T(8,128)} %project.1.after_ref), calls=%async_computation | async-start | bytes 262144 | tf_op jit(solution)/shard_map/all_to_all | solution.py:229
  25.3 0.7 %copy-start = (f32[4,8,1024]{2,1,0:T(8,128)}, f32[4,8,1024]{2,1,0:T(8,128)S(1)}, u32[]{:S(2)}) copy-start(f32[4,8,1024]{2,1,0:T(8,128)S(1)} %all-to-all-done.part_ref) | copy-start | bytes 393220
  29.8 11.5 %copy-start.6 = (f32[5,16,128]{2,1,0:T(8,128)S(1)}, f32[5,16,128]{2,1,0:T(8,128)}, u32[]{:S(2)}) copy-start(f32[5,16,128]{2,1,0:T(8,128)} %get-tuple-element.9) | copy-start | bytes 122884
  29.8 16.7 %copy-start.5 = (f32[5,16,128]{2,1,0:T(8,128)S(1)}, f32[5,16,128]{2,1,0:T(8,128)}, u32[]{:S(2)}) copy-start(f32[5,16,128]{2,1,0:T(8,128)} %get-tuple-element.10) | copy-start | bytes 122884
  29.9 18.6 %copy-start.3 = (f32[1,3,5,5]{3,0,2,1:T(1,128)S(1)}, f32[1,3,5,5]{3,0,2,1:T(1,128)}, u32[]{:S(2)}) copy-start(f32[1,3,5,5]{3,0,2,1:T(1,128)} %param.17) | copy-start | bytes 904
  29.9 28.6 %all-to-all-start.1 = ((f32[128,1,256]{2,1,0:T(1,128)}), f32[128,1,256]{2,1,0:T(1,128)S(1)}, u32[]{:S(2)}, u32[]{:S(2)}) async-start(f32[128,1,256]{2,1,0:T(1,128)} %copy.16), calls=%async_computation.1 | async-start | bytes 262144 | tf_op jit(solution)/shard_map/all_to_all | solution.py:246
  41.3 7.7 %collective-permute-start = (f32[5,16,128]{2,1,0:T(8,128)S(1)}, f32[5,16,128]{2,1,0:T(8,128)S(1)}, u32[]{:S(2)}, u32[]{:S(2)}) collective-permute-start(f32[5,16,128]{2,1,0:T(8,128)S(1)} %copy-done.6), channel_id=1, source_target_pairs={{4,0},{8,4},{12,8},{16,12},{20,16},{24,20},{28,24},{32,28},{36,32}... | collective-permute-start | bytes 122888 | tf_op jit(solution)/shard_map/ppermute | solution.py:249
  46.5 9.5 %collective-permute-start.1 = (f32[5,16,128]{2,1,0:T(8,128)S(1)}, f32[5,16,128]{2,1,0:T(8,128)S(1)}, u32[]{:S(2)}, u32[]{:S(2)}) collective-permute-start(f32[5,16,128]{2,1,0:T(8,128)S(1)} %copy-done.5), channel_id=1, source_target_pairs={{0,4},{4,8},{8,12},{12,16},{16,20},{20,24},{24,28},{28,32},{32,36}... | collective-permute-start | bytes 122888 | tf_op jit(solution)/shard_map/ppermute | solution.py:248
  49.1 7.0 %copy-start.1 = (f32[5,16,128]{2,1,0:T(8,128)}, f32[5,16,128]{2,1,0:T(8,128)S(1)}, u32[]{:S(2)}) copy-start(f32[5,16,128]{2,1,0:T(8,128)S(1)} %collective-permute-done.next_ref) | copy-start | bytes 122884
  56.1 0.6 copy-start.2

commit v2 on v1

v2 whole, which is shorter than its diff:
```python
import jax
import jax.numpy as jnp
from jax import lax
from jax.experimental import pallas as pl
from jax.experimental.pallas import tpu as pltpu
from jax.sharding import PartitionSpec as P

TILE = 128
COMP = 5
CAP = 32
SMOOTHING = 0.25
F32 = jnp.float32
BF16 = jnp.bfloat16
NT = (((1,), (1,)), ((), ()))

VMEM = pl.BlockSpec(memory_space=pltpu.MemorySpace.VMEM)
SMEM = pl.BlockSpec(memory_space=pltpu.MemorySpace.SMEM)
ANY = pl.BlockSpec(memory_space=pl.ANY)


def iota(shape, dim):
    return lax.broadcasted_iota(jnp.int32, shape, dim)


def project(hist_ref, ret_ref, amp_hbm, weight_hbm, adj_hbm, out_ref, head_ref, tail_ref, amp_ref, weight_ref, adj_ref, sems):
    moves = [
        pltpu.make_async_copy(source, target, sems.at[i])
        for i, (source, target) in enumerate(((weight_hbm, weight_ref), (amp_hbm, amp_ref), (adj_hbm, adj_ref)))
    ]
    for move in moves:
        move.start()
    group = lax.axis_index("obs")
    observers = hist_ref.shape[0]
    tiles = ret_ref.shape[0]
    hist = hist_ref[...].astype(F32)
    rows = tiles * observers
    column = [jnp.concatenate([hist[:, j * 128 : (j + 1) * 128]] * tiles, axis=0) for j in range(3)]
    eye = iota((observers, observers), 0) == iota((observers, observers), 1)
    shift = jnp.concatenate(
        [
            jnp.broadcast_to(
                jnp.sum(jnp.where(eye, ret_ref[t : t + 1, :].astype(F32), 0.0), axis=1, keepdims=True), (observers, 128)
            )
            for t in range(tiles)
        ],
        axis=0,
    ).astype(jnp.int32)
    lane = iota((rows, 128), 1)
    far = shift >= 128
    column = [
        jnp.where(far, column[1], column[0]),
        jnp.where(far, column[2], column[1]),
        column[2],
    ]
    for amount in (64, 32, 16, 8, 4, 2, 1):
        turned = [pltpu.roll(x, 128 - amount, 1) for x in column]
        stays = lane < 128 - amount
        chosen = (shift & amount) != 0
        column = [
            jnp.where(chosen, jnp.where(stays, turned[0], turned[1]), column[0]),
            jnp.where(chosen, jnp.where(stays, turned[1], turned[2]), column[1]),
            jnp.where(chosen, turned[2], column[2]),
        ]
    window = jnp.concatenate(column[:2], axis=1).astype(BF16)
    for move in moves:
        move.wait()
    copies = out_ref.shape[0]
    for t in range(tiles):
        span = slice(t * TILE, (t + 1) * TILE)
        projected = lax.dot_general(
            window[t * observers : (t + 1) * observers],
            weight_ref[span, :],
            NT,
            preferred_element_type=F32,
        )
        for c in range(COMP):
            total = jnp.sum(amp_ref[c, :, span].astype(F32) * projected, axis=0, keepdims=True)
            for copy in range(copies):
                out_ref[copy, c * tiles + t : c * tiles + t + 1, :] = total
    azimuths, radii = adj_ref.shape[1:3]
    head_ref[...] = adj_ref[:, 0]
    tail_ref[...] = adj_ref[:, azimuths - 1]
    for c in range(COMP):
        for a in range(azimuths):
            place = COMP * tiles + c * azimuths + a
            for copy in range(copies):
                up = jnp.full((1, 128), copy, jnp.int32) > group
                out_ref[copy, place : place + 1, :] = jnp.where(
                    up, adj_ref[c, a, radii - 1 : radii, :], adj_ref[c, a, 0:1, :]
                )
    for copy in range(copies):
        out_ref[copy, 50:56, :] = jnp.zeros((6, 128), F32)


def order(after_ref, block_ref, same_ref, slot_ref):
    chunks, width = block_ref.shape
    blocks = 128
    mark = jnp.where((iota((width, 2 * width), 0) < iota((width, 2 * width), 1)), 1.0, 0.0).astype(BF16)
    before = jnp.zeros((blocks, width), F32)
    for j in range(chunks):
        same = iota((blocks, width), 0) == block_ref[j : j + 1, :]
        marked = jnp.where(same, 1.0, 0.0).astype(BF16)
        same_ref[j] = marked
        counted = jnp.dot(marked, mark, preferred_element_type=F32)
        rank = jnp.sum(jnp.where(same, counted[:, :width] + before, 0.0), axis=0, keepdims=True)
        slot_ref[j] = jnp.where(iota((CAP, width), 0).astype(F32) == rank, 1.0, 0.0).astype(BF16)
        before = before + counted[:, width:]


def pack(part_ref, same_ref, slot_ref, cell_ref, source_ref, out_ref):
    chunks, width = cell_ref.shape
    count = COMP * chunks
    source = part_ref[0, :count, :]
    for group in range(1, part_ref.shape[0]):
        source = source + part_ref[group, :count, :]
    for c in range(COMP):
        for j in range(chunks):
            source_ref[c : c + 1, j * width : (j + 1) * width] = source[c * chunks + j : c * chunks + j + 1, :]
    lines = jnp.concatenate([source, cell_ref[...].astype(F32)], axis=0)
    high = lines.astype(BF16).astype(F32)
    low = lines - high
    total = jnp.zeros((128, (COMP + 1) * CAP), F32)
    for j in range(chunks):
        slot = slot_ref[j]
        placed = []
        for part in (high, low):
            placed.append(
                jnp.concatenate(
                    [
                        jnp.broadcast_to(part[c * chunks + j : c * chunks + j + 1, :], (CAP, width)).astype(BF16) * slot
                        for c in range(COMP + 1)
                    ],
                    axis=0,
                )
            )
        same = same_ref[j]
        total = total + lax.dot_general(
            jnp.concatenate([same, same], axis=1),
            jnp.concatenate(placed, axis=1),
            NT,
            preferred_element_type=F32,
        )
    out_ref[:, :128] = total[:, :128]
    out_ref[:, 128:] = jnp.concatenate([total[:, 128:], jnp.zeros((128, 64), F32)], axis=1)


def stencil(part_ref, next_ref, prev_ref, adj_ref, step_ref, jac_ref, out_ref):
    group = lax.axis_index("obs")
    groups = part_ref.shape[0]
    azimuths, radii, length = adj_ref.shape[1:]
    row = iota((radii, length), 0)
    lane = iota((radii, length), 1)
    below = jnp.maximum(group - 1, 0)
    above = jnp.minimum(group + 1, groups - 1)
    has_below = jnp.where(group > 0, 1.0, 0.0)
    has_above = jnp.where(group < groups - 1, 1.0, 0.0)
    uppers = part_ref[above, 40:56, :] * has_above
    lowers = part_ref[below, 40:56, :] * has_below
    for a in range(azimuths):
        centre = [adj_ref[c, a] for c in range(COMP)]
        pairs = [[], [], []]
        for c in range(COMP):
            x = centre[c]
            ahead = next_ref[c] if a == azimuths - 1 else adj_ref[c, a + 1]
            behind = prev_ref[c] if a == 0 else adj_ref[c, a - 1]
            pairs[0].append((ahead, behind))
            place = c * azimuths + a
            upper = uppers[place : place + 1]
            lower = lowers[place : place + 1]
            pairs[1].append(
                (
                    jnp.where(row == radii - 1, upper, pltpu.roll(x, radii - 1, 0)),
                    jnp.where(row == 0, lower, pltpu.roll(x, 1, 0)),
                )
            )
            pairs[2].append(
                (
                    jnp.where(lane == length - 1, 0.0, pltpu.roll(x, length - 1, 1)),
                    jnp.where(lane == 0, 0.0, pltpu.roll(x, 1, 1)),
                )
            )
        differences = [[f - b for f, b in pairs[d]] for d in range(3)]
        for c in range(COMP):
            rotated = jnp.zeros((radii, length), F32)
            spread = -6.0 * centre[c]
            for d in range(3):
                spread = spread + (pairs[d][c][0] + pairs[d][c][1])
                for k in range(COMP):
                    rotated = rotated + jac_ref[d, k, 0, c] * differences[d][k]
            summed = 0.5 * rotated + SMOOTHING * spread
            out_ref[c, a] = centre[c] + step_ref[a] * summed


def land(got_ref, base_ref, out_ref):
    group = lax.axis_index("obs")
    azimuths, radii, length = base_ref.shape[1:]
    radii_all = radii * lax.axis_size("obs")
    local_rows = azimuths * radii
    got = jnp.concatenate([got_ref[:, :128].T, got_ref[:, 128:].T], axis=0)
    sources = got_ref.shape[0]
    high = got.astype(BF16).astype(F32)
    low = got - high
    cell = got[COMP * CAP : (COMP + 1) * CAP].astype(jnp.int32)
    cell_row = cell >> 7
    cell_lane = cell & 127
    local = iota((local_rows, sources), 0)
    wanted = (local // radii) * radii_all + local % radii + group * radii
    total = jnp.zeros((2 * COMP * local_rows, length), F32)
    for first in range(0, CAP, 2):
        values, lanes = [], []
        for k in (first, first + 1):
            here = jnp.where(wanted == cell_row[k : k + 1], 1.0, 0.0).astype(BF16)
            values.append(
                jnp.concatenate(
                    [
                        jnp.broadcast_to(part[c * CAP + k : c * CAP + k + 1], (local_rows, sources)).astype(BF16) * here
                        for part in (high, low)
                        for c in range(COMP)
                    ],
                    axis=0,
                )
            )
            lanes.append(jnp.where(iota((length, sources), 0) == cell_lane[k : k + 1], 1.0, 0.0).astype(BF16))
        total = total + lax.dot_general(
            jnp.concatenate(values, axis=1), jnp.concatenate(lanes, axis=1), NT, preferred_element_type=F32
        )
    half = COMP * local_rows
    for c in range(COMP):
        for a in range(azimuths):
            start = (c * azimuths + a) * radii
            out_ref[c, a] = base_ref[c, a] + (total[start : start + radii] + total[half + start : half + start + radii])


def near(x):
    return pltpu.with_memory_space_constraint(x, pltpu.VMEM)


def on_device(
    histories, amplitude, weights, retarded, owner_block, owner_cell, adjoint, step_size, jacobian
):
    groups = lax.axis_size("obs")
    count = lax.axis_size("cells")
    panels = weights.shape[0]
    chunks = panels // TILE
    blocks2 = owner_block.reshape(chunks, TILE)
    cells2 = owner_cell.reshape(chunks, TILE)
    amp = amplitude.transpose(1, 0, 2)
    edge = pltpu.VMEM((COMP,) + adjoint.shape[2:], F32)

    partial_copies, head, tail = pl.pallas_call(
        project,
        out_shape=(pltpu.VMEM((groups, 56, TILE), F32), edge, edge),
        in_specs=[VMEM, VMEM, ANY, ANY, ANY],
        out_specs=(VMEM, VMEM, VMEM),
        scratch_shapes=[
            pltpu.VMEM(amp.shape, BF16),
            pltpu.VMEM(weights.shape, BF16),
            pltpu.VMEM(adjoint.shape, F32),
            pltpu.SemaphoreType.DMA((3,)),
        ],
        name="project",
    )(histories, retarded.T, amp, weights, adjoint)
    parts = lax.all_to_all(partial_copies, "obs", split_axis=0, concat_axis=0, tiled=True)
    behind = lax.ppermute(tail, "cells", [(i, (i + 1) % count) for i in range(count)])
    ahead = lax.ppermute(head, "cells", [((i + 1) % count, i) for i in range(count)])

    same, slot = pl.pallas_call(
        order,
        out_shape=(pltpu.VMEM((chunks, 128, TILE), BF16), pltpu.VMEM((chunks, CAP, TILE), BF16)),
        in_specs=[ANY, VMEM],
        out_specs=(VMEM, VMEM),
        name="order",
    )(partial_copies, blocks2)
    parts, ahead, behind = lax.optimization_barrier((parts, ahead, behind))
    panel_source, outgoing = pl.pallas_call(
        pack,
        out_shape=(jax.ShapeDtypeStruct((COMP, panels), F32), pltpu.VMEM((count, 256), F32)),
        in_specs=[VMEM] * 4,
        out_specs=(VMEM, VMEM),
        name="pack",
    )(near(parts), near(same), near(slot), cells2)
    received = lax.all_to_all(outgoing, "cells", split_axis=0, concat_axis=0, tiled=True)

    base = pl.pallas_call(
        stencil,
        out_shape=pltpu.VMEM(adjoint.shape, F32),
        in_specs=[VMEM] * 5 + [SMEM],
        out_specs=VMEM,
        name="stencil",
    )(near(parts), near(ahead), near(behind), adjoint, step_size, jacobian.transpose(1, 2, 0, 3))
    adjoint_next = pl.pallas_call(
        land,
        out_shape=jax.ShapeDtypeStruct(adjoint.shape, F32),
        in_specs=[VMEM] * 2,
        out_specs=VMEM,
        name="land",
    )(near(received), near(base))
    return adjoint_next, panel_source


def solution(mesh):
    return jax.shard_map(
        on_device,
        mesh=mesh,
        in_specs=(
            P("obs", None),
            P("obs", None, "cells"),
            P("cells", None),
            P("obs", "cells"),
            P("cells"),
            P("cells"),
            P(None, "cells", "obs", None),
            P("cells", "obs", None),
            P("cells", None, None, None),
        ),
        out_specs=(P(None, "cells", "obs", None), P(None, "cells")),
        check_vma=False,
    )
```

time: 62.2 us -> 53.4 us (0.86)
  the two profiles are of different devices: /device:TPU:32 before, /device:TPU:1 now
where the time goes in v2:
time: 53.4 us; the launch traced here: 52.9 us
  starting transfers between devices  29 us (54%)
  waiting for transfers between devices  14.6 us (27%)
  Pallas kernels  7.76 us (15%)
  local copies, waits for them, and re-layouts  0.79 us (1%)
  between operations  0.69 us (1%)
    all_to_all x1, starting transfers between devices, on_device(): lax.all_to_all(outgoing, 'cells', split_axis=0, concat_axis=0, tiled=True)  12.3 us
    all_to_all x1, starting transfers between devices, on_device(): lax.all_to_all(partial_copies, 'obs', split_axis=0, concat_axis=0, tiled=...  10.8 us
    all_to_all x1, waiting for transfers between devices, on_device(): lax.all_to_all(outgoing, 'cells', split_axis=0, concat_axis=0, tiled=True)  10.3 us
    ppermute x1, waiting for transfers between devices, on_device(): lax.ppermute(tail, 'cells', [(i, (i + 1) % count) for i in range(count)])  4.3 us
    ppermute x1, starting transfers between devices, on_device(): lax.ppermute(tail, 'cells', [(i, (i + 1) % count) for i in range(count)])  3 us
    ppermute x1, starting transfers between devices, on_device(): lax.ppermute(head, 'cells', [((i + 1) % count, i) for i in range(count)])  2.85 us
    pallas_call x1, Pallas kernels, on_device(): pl.pallas_call(project, out_shape=(pltpu.VMEM((groups, 56, TILE), F32), e...  2.76 us
    pallas_call x1, Pallas kernels, on_device(): pl.pallas_call(land, out_shape=jax.ShapeDtypeStruct(adjoint.shape, F32),...  1.58 us
  transfers between devices with their start and end apart: 4, of which 2 were waited for; matrix products, arithmetic and copies ran while one was open for 0% of the time, Pallas kernels for 4%

profile of v2, /device:TPU:1, one launch (start us, length us, event | category | flops | bytes accessed | tf_op | source)
XLA Modules:
  0.0 52.9 jit_solution(13594591722899486100)
XLA Ops:
  0.6 2.8 %project.1 = (f32[4,56,128]{2,1,0:T(8,128)}, f32[5,16,128]{2,1,0:T(8,128)S(1)}, f32[5,16,128]{2,1,0:T(8,128)S(1)}) custom-call(bf16[16,384]{1,0:T(8,128)(2,1)} %hist_ref.1, s32[8,16]{1,0:T(8,128)} %bitcast.13, bf16[5,16,1024]{2,1,0:T(8,128)(2,1)} %bitcast.11, bf16[1024,256]{1,0:T(8,128)(2,1)} %weight_hbm.1, f32[5,2,16,128]{3,2,1,0:T(8,128)} %adj_ref.1), custom_call_target="tpu_custom_call" | custom-call | tf_op jit(solution)/shard_map/project/pallas_call | solution.py:250
  3.4 10.8 %all-to-all-start = ((f32[4,56,128]{2,1,0:T(8,128)}), f32[4,56,128]{2,1,0:T(8,128)S(1)}, u32[]{:S(2)}, u32[]{:S(2)}) async-start(f32[4,56,128]{2,1,0:T(8,128)} %get-tuple-element.12.after_ref), calls=%async_computation | async-start | bytes 229376 | tf_op jit(solution)/shard_map/all_to_all | solution.py:263
  14.2 2.9 %collective-permute-start = (f32[5,16,128]{2,1,0:T(8,128)S(1)}, f32[5,16,128]{2,1,0:T(8,128)S(1)}, u32[]{:S(2)}, u32[]{:S(2)}) collective-permute-start(f32[5,16,128]{2,1,0:T(8,128)S(1)} %get-tuple-element.13), channel_id=1, source_target_pairs={{4,0},{8,4},{12,8},{16,12},{20,16},{24,20},{28,24},{32,28},{36,32}... | collective-permute-start | bytes 122888 | tf_op jit(solution)/shard_map/ppermute | solution.py:265
  17.1 3.0 %collective-permute-start.1 = (f32[5,16,128]{2,1,0:T(8,128)S(1)}, f32[5,16,128]{2,1,0:T(8,128)S(1)}, u32[]{:S(2)}, u32[]{:S(2)}) collective-permute-start(f32[5,16,128]{2,1,0:T(8,128)S(1)} %get-tuple-element.14), channel_id=1, source_target_pairs={{0,4},{4,8},{8,12},{12,16},{16,20},{20,24},{24,28},{28,32},{32,36}... | collective-permute-start | bytes 122888 | tf_op jit(solution)/shard_map/ppermute | solution.py:264
  20.1 1.0 %order.1 = (bf16[8,128,128]{2,1,0:T(8,128)(2,1)S(1)}, bf16[8,32,128]{2,1,0:T(8,128)(2,1)S(1)}) custom-call(f32[4,56,128]{2,1,0:T(8,128)} %get-tuple-element.12.after_ref, s32[8,128]{1,0:T(8,128)} %bitcast.15), custom_call_target="tpu_custom_call" | custom-call | tf_op jit(solution)/shard_map/order/pallas_call | solution.py:267
  21.1 0.0 collective-permute-done.next_ref
  21.2 4.3 %collective-permute-done.1.prev_ref = f32[5,16,128]{2,1,0:T(8,128)S(1)} collective-permute-done((f32[5,16,128]{2,1,0:T(8,128)S(1)}, f32[5,16,128]{2,1,0:T(8,128)S(1)}, u32[]{:S(2)}, u32[]{:S(2)}) %collective-permute-start.1) | collective-permute-done | bytes 40992 | tf_op jit(solution)/shard_map/ppermute | solution.py:264
  25.5 0.0 all-to-all-done.part_ref
  25.5 1.3 %pack.1 = (f32[5,1024]{1,0:T(8,128)}, f32[128,256]{1,0:T(8,128)S(1)}) custom-call(f32[4,56,128]{2,1,0:T(8,128)S(1)} %all-to-all-done.part_ref, bf16[8,128,128]{2,1,0:T(8,128)(2,1)S(1)} %get-tuple-element.16.same_ref, bf16[8,32,128]{2,1,0:T(8,128)(2,1)S(1)} %get-tuple-element.17.slot_ref, s32[8,128]{1,0:T(8,128)} %bitcast.14), custom_call_target="tpu_custom_call" | custom-call | tf_op jit(solution)/shard_map/pack/pallas_call | solution.py:275
  26.8 0.8 %copy.11 = f32[128,1,256]{2,1,0:T(1,128)} copy(f32[128,1,256]{2,0,1:T(8,128)S(1)} %bitcast.10) | data formatting | bytes 262144 | tf_op jit(solution)/shard_map/all_to_all | solution.py:282
  27.6 12.3 %all-to-all-start.1 = ((f32[128,1,256]{2,1,0:T(1,128)}), f32[128,1,256]{2,1,0:T(1,128)S(1)}, u32[]{:S(2)}, u32[]{:S(2)}) async-start(f32[128,1,256]{2,1,0:T(1,128)} %copy.11), calls=%async_computation.1 | async-start | bytes 262144 | tf_op jit(solution)/shard_map/all_to_all | solution.py:282
  39.9 1.1 %stencil.1.base_ref = f32[5,2,16,128]{3,2,1,0:T(8,128)S(1)} custom-call(f32[4,56,128]{2,1,0:T(8,128)S(1)} %all-to-all-done.part_ref, f32[5,16,128]{2,1,0:T(8,128)S(1)} %collective-permute-done.next_ref, f32[5,16,128]{2,1,0:T(8,128)S(1)} %collective-permute-done.1.prev_ref, f32[5,2,16,128]{3,2,1,0:T(8,128)} %adj_ref.1, f32[2,16,128]{2,1,0:T(8,128)} %step_ref.1, ...), custom_call_target="tpu_custom_call" | custom-call | tf_op jit(solution)/shard_map/stencil/pallas_call | solution.py:284
  41.0 10.3 %all-to-all-done.1 = f32[128,1,256]{2,1,0:T(1,128)S(1)} async-done(((f32[128,1,256]{2,1,0:T(1,128)}), f32[128,1,256]{2,1,0:T(1,128)S(1)}, u32[]{:S(2)}, u32[]{:S(2)}) %all-to-all-start.1) | async-done | bytes 131104 | tf_op jit(solution)/shard_map/all_to_all | solution.py:282
  51.4 1.6 %land.1 = f32[5,2,16,128]{3,2,1,0:T(8,128)} custom-call(f32[128,256]{1,0:T(8,128)S(1)} %bitcast.9, f32[5,2,16,128]{3,2,1,0:T(8,128)S(1)} %stencil.1.base_ref), custom_call_target="tpu_custom_call" | custom-call | tf_op jit(solution)/shard_map/land/pallas_call | solution.py:291
  (1 shorter events, 0.0 us)
Async XLA Ops:
  3.4 22.1 %all-to-all-start = ((f32[4,56,128]{2,1,0:T(8,128)}), f32[4,56,128]{2,1,0:T(8,128)S(1)}, u32[]{:S(2)}, u32[]{:S(2)}) async-start(f32[4,56,128]{2,1,0:T(8,128)} %get-tuple-element.12.after_ref), calls=%async_computation | async-start | bytes 229376 | tf_op jit(solution)/shard_map/all_to_all | solution.py:263
  14.2 6.9 %collective-permute-start = (f32[5,16,128]{2,1,0:T(8,128)S(1)}, f32[5,16,128]{2,1,0:T(8,128)S(1)}, u32[]{:S(2)}, u32[]{:S(2)}) collective-permute-start(f32[5,16,128]{2,1,0:T(8,128)S(1)} %get-tuple-element.13), channel_id=1, source_target_pairs={{4,0},{8,4},{12,8},{16,12},{20,16},{24,20},{28,24},{32,28},{36,32}... | collective-permute-start | bytes 122888 | tf_op jit(solution)/shard_map/ppermute | solution.py:265
  17.1 8.3 %collective-permute-start.1 = (f32[5,16,128]{2,1,0:T(8,128)S(1)}, f32[5,16,128]{2,1,0:T(8,128)S(1)}, u32[]{:S(2)}, u32[]{:S(2)}) collective-permute-start(f32[5,16,128]{2,1,0:T(8,128)S(1)} %get-tuple-element.14), channel_id=1, source_target_pairs={{0,4},{4,8},{8,12},{12,16},{16,20},{20,24},{24,28},{28,32},{32,36}... | collective-permute-start | bytes 122888 | tf_op jit(solution)/shard_map/ppermute | solution.py:264
  27.6 23.8 %all-to-all-start.1 = ((f32[128,1,256]{2,1,0:T(1,128)}), f32[128,1,256]{2,1,0:T(1,128)S(1)}, u32[]{:S(2)}, u32[]{:S(2)}) async-start(f32[128,1,256]{2,1,0:T(1,128)} %copy.11), calls=%async_computation.1 | async-start | bytes 262144 | tf_op jit(solution)/shard_map/all_to_all | solution.py:282

commit v3 on v2

--- a/solution.py
+++ b/solution.py
@@ -4,6 +4,7 @@
 from jax.experimental import pallas as pl
 from jax.experimental.pallas import tpu as pltpu
 from jax.sharding import PartitionSpec as P
+
 
 TILE = 128
 COMP = 5
@@ -92,10 +93,11 @@
         out_ref[copy, 50:56, :] = jnp.zeros((6, 128), F32)
 
 
-def order(after_ref, block_ref, same_ref, slot_ref):
+def order(after_ref, block_ref, cell_ref, same_ref, slot_ref, line_ref):
     chunks, width = block_ref.shape
     blocks = 128
     mark = jnp.where((iota((width, 2 * width), 0) < iota((width, 2 * width), 1)), 1.0, 0.0).astype(BF16)
+    line_ref[...] = cell_ref[...].astype(F32)
     before = jnp.zeros((blocks, width), F32)
     for j in range(chunks):
         same = iota((blocks, width), 0) == block_ref[j : j + 1, :]
@@ -107,16 +109,16 @@
         before = before + counted[:, width:]
 
 
-def pack(part_ref, same_ref, slot_ref, cell_ref, source_ref, out_ref):
-    chunks, width = cell_ref.shape
-    count = COMP * chunks
+def whole_source(part_ref, count):
     source = part_ref[0, :count, :]
     for group in range(1, part_ref.shape[0]):
         source = source + part_ref[group, :count, :]
-    for c in range(COMP):
-        for j in range(chunks):
-            source_ref[c : c + 1, j * width : (j + 1) * width] = source[c * chunks + j : c * chunks + j + 1, :]
-    lines = jnp.concatenate([source, cell_ref[...].astype(F32)], axis=0)
+    return source
+
+
+def pack(part_ref, same_ref, slot_ref, line_ref, out_ref):
+    chunks, width = line_ref.shape
+    lines = jnp.concatenate([whole_source(part_ref, COMP * chunks), line_ref[...]], axis=0)
     high = lines.astype(BF16).astype(F32)
     low = lines - high
     total = jnp.zeros((128, (COMP + 1) * CAP), F32)
@@ -140,11 +142,16 @@
             NT,
             preferred_element_type=F32,
         )
-    out_ref[:, :128] = total[:, :128]
-    out_ref[:, 128:] = jnp.concatenate([total[:, 128:], jnp.zeros((128, 64), F32)], axis=1)
-
-
-def stencil(part_ref, next_ref, prev_ref, adj_ref, step_ref, jac_ref, out_ref):
+    rest = jnp.concatenate([total[:, 128:], jnp.zeros((128, 64), F32)], axis=1)
+    out_ref[:, 0, :] = jnp.concatenate([total[:, :128], rest], axis=1)
+
+
+def stencil(part_ref, next_ref, prev_ref, adj_ref, step_ref, jac_ref, out_ref, source_ref):
+    chunks = source_ref.shape[1] // TILE
+    source = whole_source(part_ref, COMP * chunks)
+    for c in range(COMP):
+        for j in range(chunks):
+            source_ref[c : c + 1, j * TILE : (j + 1) * TILE] = source[c * chunks + j : c * chunks + j + 1, :]
     group = lax.axis_index("obs")
     groups = part_ref.shape[0]
     azimuths, radii, length = adj_ref.shape[1:]
@@ -264,28 +271,31 @@
     behind = lax.ppermute(tail, "cells", [(i, (i + 1) % count) for i in range(count)])
     ahead = lax.ppermute(head, "cells", [((i + 1) % count, i) for i in range(count)])
 
-    same, slot = pl.pallas_call(
+    same, slot, lines = pl.pallas_call(
         order,
-        out_shape=(pltpu.VMEM((chunks, 128, TILE), BF16), pltpu.VMEM((chunks, CAP, TILE), BF16)),
-        in_specs=[ANY, VMEM],
+        out_shape=(
+            pltpu.VMEM((chunks, 128, TILE), BF16),
+            pltpu.VMEM((chunks, CAP, TILE), BF16),
+            pltpu.VMEM((chunks, TILE), F32),
+        ),
+        in_specs=[ANY, VMEM, VMEM],
+        out_specs=(VMEM, VMEM, VMEM),
+        name="order",
+    )(partial_copies, blocks2, cells2)
+    outgoing = pl.pallas_call(
+        pack,
+        out_shape=jax.ShapeDtypeStruct((count, 1, 256), F32),
+        in_specs=[VMEM] * 4,
+        out_specs=VMEM,
+        name="pack",
+    )(near(parts), near(same), near(slot), near(lines))
+    received = lax.all_to_all(outgoing, "cells", split_axis=0, concat_axis=0, tiled=True)
+
+    base, panel_source = pl.pallas_call(
+        stencil,
+        out_shape=(pltpu.VMEM(adjoint.shape, F32), jax.ShapeDtypeStruct((COMP, panels), F32)),
+        in_specs=[VMEM] * 5 + [SMEM],
         out_specs=(VMEM, VMEM),
-        name="order",
-    )(partial_copies, blocks2)
-    parts, ahead, behind = lax.optimization_barrier((parts, ahead, behind))
-    panel_source, outgoing = pl.pallas_call(
-        pack,
-        out_shape=(jax.ShapeDtypeStruct((COMP, panels), F32), pltpu.VMEM((count, 256), F32)),
-        in_specs=[VMEM] * 4,
-        out_specs=(VMEM, VMEM),
-        name="pack",
-    )(near(parts), near(same), near(slot), cells2)
-    received = lax.all_to_all(outgoing, "cells", split_axis=0, concat_axis=0, tiled=True)
-
-    base = pl.pallas_call(
-        stencil,
-        out_shape=pltpu.VMEM(adjoint.shape, F32),
-        in_specs=[VMEM] * 5 + [SMEM],
-        out_specs=VMEM,
         name="stencil",
     )(near(parts), near(ahead), near(behind), adjoint, step_size, jacobian.transpose(1, 2, 0, 3))
     adjoint_next = pl.pallas_call(
@@ -294,7 +304,7 @@
         in_specs=[VMEM] * 2,
         out_specs=VMEM,
         name="land",
-    )(near(received), near(base))
+    )(near(received.reshape(count, 256)), near(base))
     return adjoint_next, panel_source
 
 

time: 53.4 us -> 53.8 us (level)
  the two profiles are of different devices: /device:TPU:1 before, /device:TPU:32 now
where the time goes in v3:
time: 53.8 us; the launch traced here: 53.3 us
  starting transfers between devices  29 us (54%)
  waiting for transfers between devices  15.5 us (29%)
  Pallas kernels  8.13 us (15%)
  between operations  0.68 us (1%)
    all_to_all x1, starting transfers between devices, on_device(): lax.all_to_all(outgoing, 'cells', split_axis=0, concat_axis=0, tiled=True)  11.6 us
    all_to_all x1, starting transfers between devices, on_device(): lax.all_to_all(partial_copies, 'obs', split_axis=0, concat_axis=0, tiled=...  10.3 us
    all_to_all x1, waiting for transfers between devices, on_device(): lax.all_to_all(partial_copies, 'obs', split_axis=0, concat_axis=0, tiled=...  7.91 us
    ppermute x1, waiting for transfers between devices, on_device(): lax.ppermute(tail, 'cells', [(i, (i + 1) % count) for i in range(count)])  7.6 us
    ppermute x1, starting transfers between devices, on_device(): lax.ppermute(head, 'cells', [((i + 1) % count, i) for i in range(count)])  5.19 us
    pallas_call x1, Pallas kernels, on_device(): pl.pallas_call(project, out_shape=(pltpu.VMEM((groups, 56, TILE), F32), e...  2.76 us
    ppermute x1, starting transfers between devices, on_device(): lax.ppermute(tail, 'cells', [(i, (i + 1) % count) for i in range(count)])  1.92 us
    pallas_call x1, Pallas kernels, on_device(): pl.pallas_call(stencil, out_shape=(pltpu.VMEM(adjoint.shape, F32), jax.Sh...  1.7 us
  transfers between devices with their start and end apart: 4, of which 2 were waited for; matrix products, arithmetic and copies ran while one was open for 0% of the time, Pallas kernels for 5%

profile of v3, /device:TPU:32, one launch (start us, length us, event | category | flops | bytes accessed | tf_op | source)
XLA Modules:
  0.0 53.3 jit_solution(4869860859987197879)
XLA Ops:
  0.6 2.8 %project.1 = (f32[4,56,128]{2,1,0:T(8,128)}, f32[5,16,128]{2,1,0:T(8,128)S(1)}, f32[5,16,128]{2,1,0:T(8,128)S(1)}) custom-call(bf16[16,384]{1,0:T(8,128)(2,1)} %hist_ref.1, s32[8,16]{1,0:T(8,128)} %bitcast.11, bf16[5,16,1024]{2,1,0:T(8,128)(2,1)} %bitcast.9, bf16[1024,256]{1,0:T(8,128)(2,1)} %weight_hbm.1, f32[5,2,16,128]{3,2,1,0:T(8,128)} %adj_ref.1), custom_call_target="tpu_custom_call" | custom-call | tf_op jit(solution)/shard_map/project/pallas_call | solution.py:257
  3.4 10.3 %all-to-all-start = ((f32[4,56,128]{2,1,0:T(8,128)}), f32[4,56,128]{2,1,0:T(8,128)S(1)}, u32[]{:S(2)}, u32[]{:S(2)}) async-start(f32[4,56,128]{2,1,0:T(8,128)} %get-tuple-element.10.after_ref), calls=%async_computation | async-start | bytes 229376 | tf_op jit(solution)/shard_map/all_to_all | solution.py:270
  13.7 1.0 %order.1 = (bf16[8,128,128]{2,1,0:T(8,128)(2,1)S(1)}, bf16[8,32,128]{2,1,0:T(8,128)(2,1)S(1)}, f32[8,128]{1,0:T(8,128)S(1)}) custom-call(f32[4,56,128]{2,1,0:T(8,128)} %get-tuple-element.10.after_ref, s32[8,128]{1,0:T(8,128)} %bitcast.12, s32[8,128]{1,0:T(8,128)} %bitcast.13), custom_call_target="tpu_custom_call" | custom-call | tf_op jit(solution)/shard_map/order/pallas_call | solution.py:274
  14.8 7.9 %all-to-all-done.part_ref = f32[4,56,128]{2,1,0:T(8,128)S(1)} async-done(((f32[4,56,128]{2,1,0:T(8,128)}), f32[4,56,128]{2,1,0:T(8,128)S(1)}, u32[]{:S(2)}, u32[]{:S(2)}) %all-to-all-start) | async-done | bytes 114720 | tf_op jit(solution)/shard_map/all_to_all | solution.py:270
  22.7 1.1 %pack.1 = f32[128,1,256]{2,1,0:T(1,128)} custom-call(f32[4,56,128]{2,1,0:T(8,128)S(1)} %all-to-all-done.part_ref, bf16[8,128,128]{2,1,0:T(8,128)(2,1)S(1)} %get-tuple-element.11.same_ref, bf16[8,32,128]{2,1,0:T(8,128)(2,1)S(1)} %get-tuple-element.12.slot_ref, f32[8,128]{1,0:T(8,128)S(1)} %get-tuple-element.13.line_ref), custom_call_target="tpu_custom_call" | custom-call | tf_op jit(solution)/shard_map/pack/pallas_call | solution.py:285
  23.7 11.6 %all-to-all-start.1 = ((f32[128,1,256]{2,1,0:T(1,128)}), f32[128,1,256]{2,1,0:T(1,128)S(1)}, u32[]{:S(2)}, u32[]{:S(2)}) async-start(f32[128,1,256]{2,1,0:T(1,128)} %pack.1), calls=%async_computation.1 | async-start | bytes 262144 | tf_op jit(solution)/shard_map/all_to_all | solution.py:292
  35.3 5.2 %collective-permute-start = (f32[5,16,128]{2,1,0:T(8,128)S(1)}, f32[5,16,128]{2,1,0:T(8,128)S(1)}, u32[]{:S(2)}, u32[]{:S(2)}) collective-permute-start(f32[5,16,128]{2,1,0:T(8,128)S(1)} %get-tuple-element.14), channel_id=1, source_target_pairs={{4,0},{8,4},{12,8},{16,12},{20,16},{24,20},{28,24},{32,28},{36,32}... | collective-permute-start | bytes 122888 | tf_op jit(solution)/shard_map/ppermute | solution.py:272
  40.5 1.9 %collective-permute-start.1 = (f32[5,16,128]{2,1,0:T(8,128)S(1)}, f32[5,16,128]{2,1,0:T(8,128)S(1)}, u32[]{:S(2)}, u32[]{:S(2)}) collective-permute-start(f32[5,16,128]{2,1,0:T(8,128)S(1)} %get-tuple-element.15), channel_id=1, source_target_pairs={{0,4},{4,8},{8,12},{12,16},{16,20},{20,24},{24,28},{28,32},{32,36}... | collective-permute-start | bytes 122888 | tf_op jit(solution)/shard_map/ppermute | solution.py:271
  42.4 0.0 collective-permute-done.next_ref
  42.4 7.6 %collective-permute-done.1.prev_ref = f32[5,16,128]{2,1,0:T(8,128)S(1)} collective-permute-done((f32[5,16,128]{2,1,0:T(8,128)S(1)}, f32[5,16,128]{2,1,0:T(8,128)S(1)}, u32[]{:S(2)}, u32[]{:S(2)}) %collective-permute-start.1) | collective-permute-done | bytes 40992 | tf_op jit(solution)/shard_map/ppermute | solution.py:271
  50.0 1.7 %stencil.1 = (f32[5,2,16,128]{3,2,1,0:T(8,128)S(1)}, f32[5,1024]{1,0:T(8,128)}) custom-call(f32[4,56,128]{2,1,0:T(8,128)S(1)} %all-to-all-done.part_ref, f32[5,16,128]{2,1,0:T(8,128)S(1)} %collective-permute-done.next_ref, f32[5,16,128]{2,1,0:T(8,128)S(1)} %collective-permute-done.1.prev_ref, f32[5,2,16,128]{3,2,1,0:T(8,128)} %adj_ref.1, ...), custom_call_target="tpu_custom_call" | custom-call | tf_op jit(solution)/shard_map/stencil/pallas_call | solution.py:294
  51.7 0.0 all-to-all-done.1
  51.8 1.6 %land.1 = f32[5,2,16,128]{3,2,1,0:T(8,128)} custom-call(f32[128,256]{1,0:T(8,128)S(1)} %bitcast.8, f32[5,2,16,128]{3,2,1,0:T(8,128)S(1)} %get-tuple-element.16.base_ref), custom_call_target="tpu_custom_call" | custom-call | tf_op jit(solution)/shard_map/land/pallas_call | solution.py:301
  (1 shorter events, 0.0 us)
Async XLA Ops:
  3.4 19.3 %all-to-all-start = ((f32[4,56,128]{2,1,0:T(8,128)}), f32[4,56,128]{2,1,0:T(8,128)S(1)}, u32[]{:S(2)}, u32[]{:S(2)}) async-start(f32[4,56,128]{2,1,0:T(8,128)} %get-tuple-element.10.after_ref), calls=%async_computation | async-start | bytes 229376 | tf_op jit(solution)/shard_map/all_to_all | solution.py:270
  23.7 28.0 %all-to-all-start.1 = ((f32[128,1,256]{2,1,0:T(1,128)}), f32[128,1,256]{2,1,0:T(1,128)S(1)}, u32[]{:S(2)}, u32[]{:S(2)}) async-start(f32[128,1,256]{2,1,0:T(1,128)} %pack.1), calls=%async_computation.1 | async-start | bytes 262144 | tf_op jit(solution)/shard_map/all_to_all | solution.py:292
  35.3 7.1 %collective-permute-start = (f32[5,16,128]{2,1,0:T(8,128)S(1)}, f32[5,16,128]{2,1,0:T(8,128)S(1)}, u32[]{:S(2)}, u32[]{:S(2)}) collective-permute-start(f32[5,16,128]{2,1,0:T(8,128)S(1)} %get-tuple-element.14), channel_id=1, source_target_pairs={{4,0},{8,4},{12,8},{16,12},{20,16},{24,20},{28,24},{32,28},{36,32}... | collective-permute-start | bytes 122888 | tf_op jit(solution)/shard_map/ppermute | solution.py:272
  40.5 9.5 %collective-permute-start.1 = (f32[5,16,128]{2,1,0:T(8,128)S(1)}, f32[5,16,128]{2,1,0:T(8,128)S(1)}, u32[]{:S(2)}, u32[]{:S(2)}) collective-permute-start(f32[5,16,128]{2,1,0:T(8,128)S(1)} %get-tuple-element.15), channel_id=1, source_target_pairs={{0,4},{4,8},{8,12},{12,16},{16,20},{20,24},{24,28},{28,32},{32,36}... | collective-permute-start | bytes 122888 | tf_op jit(solution)/shard_map/ppermute | solution.py:271

commit v4 on v3

--- a/solution.py
+++ b/solution.py
@@ -13,6 +13,8 @@
 F32 = jnp.float32
 BF16 = jnp.bfloat16
 NT = (((1,), (1,)), ((), ()))
+FIRST_CELL = 75
+FIRST_GROUP = 0
 
 VMEM = pl.BlockSpec(memory_space=pltpu.MemorySpace.VMEM)
 SMEM = pl.BlockSpec(memory_space=pltpu.MemorySpace.SMEM)
@@ -85,7 +87,7 @@
         for a in range(azimuths):
             place = COMP * tiles + c * azimuths + a
             for copy in range(copies):
-                up = jnp.full((1, 128), copy, jnp.int32) > group
+                up = jnp.full((1, 128), (copy + FIRST_GROUP) % copies, jnp.int32) > group
                 out_ref[copy, place : place + 1, :] = jnp.where(
                     up, adj_ref[c, a, radii - 1 : radii, :], adj_ref[c, a, 0:1, :]
                 )
@@ -98,9 +100,10 @@
     blocks = 128
     mark = jnp.where((iota((width, 2 * width), 0) < iota((width, 2 * width), 1)), 1.0, 0.0).astype(BF16)
     line_ref[...] = cell_ref[...].astype(F32)
+    named = (iota((blocks, width), 0) + FIRST_CELL) % blocks
     before = jnp.zeros((blocks, width), F32)
     for j in range(chunks):
-        same = iota((blocks, width), 0) == block_ref[j : j + 1, :]
+        same = named == block_ref[j : j + 1, :]
         marked = jnp.where(same, 1.0, 0.0).astype(BF16)
         same_ref[j] = marked
         counted = jnp.dot(marked, mark, preferred_element_type=F32)
@@ -161,8 +164,8 @@
     above = jnp.minimum(group + 1, groups - 1)
     has_below = jnp.where(group > 0, 1.0, 0.0)
     has_above = jnp.where(group < groups - 1, 1.0, 0.0)
-    uppers = part_ref[above, 40:56, :] * has_above
-    lowers = part_ref[below, 40:56, :] * has_below
+    uppers = part_ref[(above - FIRST_GROUP + groups) % groups, 40:56, :] * has_above
+    lowers = part_ref[(below - FIRST_GROUP + groups) % groups, 40:56, :] * has_below
     for a in range(azimuths):
         centre = [adj_ref[c, a] for c in range(COMP)]
         pairs = [[], [], []]
@@ -238,6 +241,10 @@
             out_ref[c, a] = base_ref[c, a] + (total[start : start + radii] + total[half + start : half + start + radii])
 
 
+def turned(size, first):
+    return [[(i + first) % size for i in range(size)]]
+
+
 def near(x):
     return pltpu.with_memory_space_constraint(x, pltpu.VMEM)
 
@@ -267,7 +274,9 @@
         ],
         name="project",
     )(histories, retarded.T, amp, weights, adjoint)
-    parts = lax.all_to_all(partial_copies, "obs", split_axis=0, concat_axis=0, tiled=True)
+    parts = lax.all_to_all(
+        partial_copies, "obs", 0, 0, axis_index_groups=turned(groups, FIRST_GROUP), tiled=True
+    )
     behind = lax.ppermute(tail, "cells", [(i, (i + 1) % count) for i in range(count)])
     ahead = lax.ppermute(head, "cells", [((i + 1) % count, i) for i in range(count)])
 
@@ -289,7 +298,9 @@
         out_specs=VMEM,
         name="pack",
     )(near(parts), near(same), near(slot), near(lines))
-    received = lax.all_to_all(outgoing, "cells", split_axis=0, concat_axis=0, tiled=True)
+    received = lax.all_to_all(
+        outgoing, "cells", 0, 0, axis_index_groups=turned(count, FIRST_CELL), tiled=True
+    )
 
     base, panel_source = pl.pallas_call(
         stencil,

time: 53.8 us -> 51.3 us (0.954)
  the two profiles are of different devices: /device:TPU:32 before, /device:TPU:8 now
where the time goes in v4:
time: 51.3 us; the launch traced here: 50.8 us
  starting transfers between devices  27.7 us (54%)
  waiting for transfers between devices  14.3 us (28%)
  Pallas kernels  8.09 us (16%)
  between operations  0.68 us (1%)
    all_to_all x1, starting transfers between devices, on_device(): lax.all_to_all(outgoing, 'cells', 0, 0, axis_index_groups=turned(count, F...  12.4 us
    all_to_all x1, starting transfers between devices, on_device(): lax.all_to_all(partial_copies, 'obs', 0, 0, axis_index_groups=turned(grou...  10.3 us
    all_to_all x1, waiting for transfers between devices, on_device(): lax.all_to_all(partial_copies, 'obs', 0, 0, axis_index_groups=turned(grou...  7.94 us
    ppermute x1, waiting for transfers between devices, on_device(): lax.ppermute(tail, 'cells', [(i, (i + 1) % count) for i in range(count)])  6.39 us
    ppermute x1, starting transfers between devices, on_device(): lax.ppermute(head, 'cells', [((i + 1) % count, i) for i in range(count)])  3.08 us
    pallas_call x1, Pallas kernels, on_device(): pl.pallas_call(project, out_shape=(pltpu.VMEM((groups, 56, TILE), F32), e...  2.76 us
    ppermute x1, starting transfers between devices, on_device(): lax.ppermute(tail, 'cells', [(i, (i + 1) % count) for i in range(count)])  1.92 us
    pallas_call x1, Pallas kernels, on_device(): pl.pallas_call(stencil, out_shape=(pltpu.VMEM(adjoint.shape, F32), jax.Sh...  1.7 us
  transfers between devices with their start and end apart: 4, of which 2 were waited for; matrix products, arithmetic and copies ran while one was open for 0% of the time, Pallas kernels for 5%

profile of v4, /device:TPU:8, one launch (start us, length us, event | category | flops | bytes accessed | tf_op | source)
XLA Modules:
  0.0 50.8 jit_solution(7660124131106160550)
XLA Ops:
  0.6 2.8 %project.1 = (f32[4,56,128]{2,1,0:T(8,128)}, f32[5,16,128]{2,1,0:T(8,128)S(1)}, f32[5,16,128]{2,1,0:T(8,128)S(1)}) custom-call(bf16[16,384]{1,0:T(8,128)(2,1)} %hist_ref.1, s32[8,16]{1,0:T(8,128)} %bitcast.11, bf16[5,16,1024]{2,1,0:T(8,128)(2,1)} %bitcast.9, bf16[1024,256]{1,0:T(8,128)(2,1)} %weight_hbm.1, f32[5,2,16,128]{3,2,1,0:T(8,128)} %adj_ref.1), custom_call_target="tpu_custom_call" | custom-call | tf_op jit(solution)/shard_map/project/pallas_call | solution.py:264
  3.4 10.3 %all-to-all-start = ((f32[4,56,128]{2,1,0:T(8,128)}), f32[4,56,128]{2,1,0:T(8,128)S(1)}, u32[]{:S(2)}, u32[]{:S(2)}) async-start(f32[4,56,128]{2,1,0:T(8,128)} %get-tuple-element.10.after_ref), calls=%async_computation | async-start | bytes 229376 | tf_op jit(solution)/shard_map/all_to_all | solution.py:277
  13.7 1.0 %order.1 = (bf16[8,128,128]{2,1,0:T(8,128)(2,1)S(1)}, bf16[8,32,128]{2,1,0:T(8,128)(2,1)S(1)}, f32[8,128]{1,0:T(8,128)S(1)}) custom-call(f32[4,56,128]{2,1,0:T(8,128)} %get-tuple-element.10.after_ref, s32[8,128]{1,0:T(8,128)} %bitcast.12, s32[8,128]{1,0:T(8,128)} %bitcast.13), custom_call_target="tpu_custom_call" | custom-call | tf_op jit(solution)/shard_map/order/pallas_call | solution.py:283
  14.7 7.9 %all-to-all-done.part_ref = f32[4,56,128]{2,1,0:T(8,128)S(1)} async-done(((f32[4,56,128]{2,1,0:T(8,128)}), f32[4,56,128]{2,1,0:T(8,128)S(1)}, u32[]{:S(2)}, u32[]{:S(2)}) %all-to-all-start) | async-done | bytes 114720 | tf_op jit(solution)/shard_map/all_to_all | solution.py:277
  22.7 1.1 %pack.1 = f32[128,1,256]{2,1,0:T(1,128)} custom-call(f32[4,56,128]{2,1,0:T(8,128)S(1)} %all-to-all-done.part_ref, bf16[8,128,128]{2,1,0:T(8,128)(2,1)S(1)} %get-tuple-element.11.same_ref, bf16[8,32,128]{2,1,0:T(8,128)(2,1)S(1)} %get-tuple-element.12.slot_ref, f32[8,128]{1,0:T(8,128)S(1)} %get-tuple-element.13.line_ref), custom_call_target="tpu_custom_call" | custom-call | tf_op jit(solution)/shard_map/pack/pallas_call | solution.py:294
  23.7 12.4 %all-to-all-start.1 = ((f32[128,1,256]{2,1,0:T(1,128)}), f32[128,1,256]{2,1,0:T(1,128)S(1)}, u32[]{:S(2)}, u32[]{:S(2)}) async-start(f32[128,1,256]{2,1,0:T(1,128)} %pack.1), calls=%async_computation.1 | async-start | bytes 262144 | tf_op jit(solution)/shard_map/all_to_all | solution.py:301
  36.1 3.1 %collective-permute-start = (f32[5,16,128]{2,1,0:T(8,128)S(1)}, f32[5,16,128]{2,1,0:T(8,128)S(1)}, u32[]{:S(2)}, u32[]{:S(2)}) collective-permute-start(f32[5,16,128]{2,1,0:T(8,128)S(1)} %get-tuple-element.14), channel_id=1, source_target_pairs={{4,0},{8,4},{12,8},{16,12},{20,16},{24,20},{28,24},{32,28},{36,32}... | collective-permute-start | bytes 122888 | tf_op jit(solution)/shard_map/ppermute | solution.py:281
  39.2 1.9 %collective-permute-start.1 = (f32[5,16,128]{2,1,0:T(8,128)S(1)}, f32[5,16,128]{2,1,0:T(8,128)S(1)}, u32[]{:S(2)}, u32[]{:S(2)}) collective-permute-start(f32[5,16,128]{2,1,0:T(8,128)S(1)} %get-tuple-element.15), channel_id=1, source_target_pairs={{0,4},{4,8},{8,12},{12,16},{16,20},{20,24},{24,28},{28,32},{32,36}... | collective-permute-start | bytes 122888 | tf_op jit(solution)/shard_map/ppermute | solution.py:280
  41.2 0.0 collective-permute-done.next_ref
  41.2 6.4 %collective-permute-done.1.prev_ref = f32[5,16,128]{2,1,0:T(8,128)S(1)} collective-permute-done((f32[5,16,128]{2,1,0:T(8,128)S(1)}, f32[5,16,128]{2,1,0:T(8,128)S(1)}, u32[]{:S(2)}, u32[]{:S(2)}) %collective-permute-start.1) | collective-permute-done | bytes 40992 | tf_op jit(solution)/shard_map/ppermute | solution.py:280
  47.6 1.7 %stencil.1 = (f32[5,2,16,128]{3,2,1,0:T(8,128)S(1)}, f32[5,1024]{1,0:T(8,128)}) custom-call(f32[4,56,128]{2,1,0:T(8,128)S(1)} %all-to-all-done.part_ref, f32[5,16,128]{2,1,0:T(8,128)S(1)} %collective-permute-done.next_ref, f32[5,16,128]{2,1,0:T(8,128)S(1)} %collective-permute-done.1.prev_ref, f32[5,2,16,128]{3,2,1,0:T(8,128)} %adj_ref.1, ...), custom_call_target="tpu_custom_call" | custom-call | tf_op jit(solution)/shard_map/stencil/pallas_call | solution.py:305
  49.3 0.0 all-to-all-done.1
  49.3 1.6 %land.1 = f32[5,2,16,128]{3,2,1,0:T(8,128)} custom-call(f32[128,256]{1,0:T(8,128)S(1)} %bitcast.8, f32[5,2,16,128]{3,2,1,0:T(8,128)S(1)} %get-tuple-element.16.base_ref), custom_call_target="tpu_custom_call" | custom-call | tf_op jit(solution)/shard_map/land/pallas_call | solution.py:312
  (1 shorter events, 0.0 us)
Async XLA Ops:
  3.4 19.3 %all-to-all-start = ((f32[4,56,128]{2,1,0:T(8,128)}), f32[4,56,128]{2,1,0:T(8,128)S(1)}, u32[]{:S(2)}, u32[]{:S(2)}) async-start(f32[4,56,128]{2,1,0:T(8,128)} %get-tuple-element.10.after_ref), calls=%async_computation | async-start | bytes 229376 | tf_op jit(solution)/shard_map/all_to_all | solution.py:277
  23.7 25.5 %all-to-all-start.1 = ((f32[128,1,256]{2,1,0:T(1,128)}), f32[128,1,256]{2,1,0:T(1,128)S(1)}, u32[]{:S(2)}, u32[]{:S(2)}) async-start(f32[128,1,256]{2,1,0:T(1,128)} %pack.1), calls=%async_computation.1 | async-start | bytes 262144 | tf_op jit(solution)/shard_map/all_to_all | solution.py:301
  36.1 5.0 %collective-permute-start = (f32[5,16,128]{2,1,0:T(8,128)S(1)}, f32[5,16,128]{2,1,0:T(8,128)S(1)}, u32[]{:S(2)}, u32[]{:S(2)}) collective-permute-start(f32[5,16,128]{2,1,0:T(8,128)S(1)} %get-tuple-element.14), channel_id=1, source_target_pairs={{4,0},{8,4},{12,8},{16,12},{20,16},{24,20},{28,24},{32,28},{36,32}... | collective-permute-start | bytes 122888 | tf_op jit(solution)/shard_map/ppermute | solution.py:281
  39.2 8.3 %collective-permute-start.1 = (f32[5,16,128]{2,1,0:T(8,128)S(1)}, f32[5,16,128]{2,1,0:T(8,128)S(1)}, u32[]{:S(2)}, u32[]{:S(2)}) collective-permute-start(f32[5,16,128]{2,1,0:T(8,128)S(1)} %get-tuple-element.15), channel_id=1, source_target_pairs={{0,4},{4,8},{8,12},{12,16},{16,20},{20,24},{24,28},{28,32},{32,36}... | collective-permute-start | bytes 122888 | tf_op jit(solution)/shard_map/ppermute | solution.py:280

commit v5 on v4

--- a/solution.py
+++ b/solution.py
@@ -14,7 +14,7 @@
 BF16 = jnp.bfloat16
 NT = (((1,), (1,)), ((), ()))
 FIRST_CELL = 75
-FIRST_GROUP = 0
+FIRST_GROUP = 2
 
 VMEM = pl.BlockSpec(memory_space=pltpu.MemorySpace.VMEM)
 SMEM = pl.BlockSpec(memory_space=pltpu.MemorySpace.SMEM)
@@ -25,16 +25,39 @@
     return lax.broadcasted_iota(jnp.int32, shape, dim)
 
 
-def project(hist_ref, ret_ref, amp_hbm, weight_hbm, adj_hbm, out_ref, head_ref, tail_ref, amp_ref, weight_ref, adj_ref, sems):
+def project(
+    hist_hbm, ret_hbm, adj_hbm, weight_hbm, amp_hbm, block_hbm, cell_hbm, step_hbm,
+    out_hbm, inner_ref, outer_ref, adj_ref, block_ref, cell_ref, step_ref,
+    hist_ref, ret_ref, weight_ref, amp_ref, part_ref, line_ref, sems,
+):
+    group = lax.axis_index("obs")
+    odd = lax.axis_index("cells") % 2
+    copies = out_hbm.shape[0]
+    tiles, observers = ret_hbm.shape
+    azimuths, radii = adj_ref.shape[1:3]
+    count = COMP * tiles
+    half = tiles * TILE // 2
     moves = [
         pltpu.make_async_copy(source, target, sems.at[i])
-        for i, (source, target) in enumerate(((weight_hbm, weight_ref), (amp_hbm, amp_ref), (adj_hbm, adj_ref)))
+        for i, (source, target) in enumerate(
+            (
+                (hist_hbm, hist_ref),
+                (ret_hbm, ret_ref),
+                (adj_hbm, adj_ref),
+                (weight_hbm.at[:half], weight_ref.at[:half]),
+                (amp_hbm.at[:, :, :half], amp_ref.at[:, :, :half]),
+                (weight_hbm.at[half:], weight_ref.at[half:]),
+                (amp_hbm.at[:, :, half:], amp_ref.at[:, :, half:]),
+                (block_hbm, block_ref),
+                (cell_hbm, cell_ref),
+                (step_hbm, step_ref),
+            )
+        )
     ]
     for move in moves:
         move.start()
-    group = lax.axis_index("obs")
-    observers = hist_ref.shape[0]
-    tiles = ret_ref.shape[0]
+    moves[0].wait()
+    moves[1].wait()
     hist = hist_ref[...].astype(F32)
     rows = tiles * observers
     column = [jnp.concatenate([hist[:, j * 128 : (j + 1) * 128]] * tiles, axis=0) for j in range(3)]
@@ -56,19 +79,39 @@
         column[2],
     ]
     for amount in (64, 32, 16, 8, 4, 2, 1):
-        turned = [pltpu.roll(x, 128 - amount, 1) for x in column]
+        rolled = [pltpu.roll(x, 128 - amount, 1) for x in column]
         stays = lane < 128 - amount
         chosen = (shift & amount) != 0
         column = [
-            jnp.where(chosen, jnp.where(stays, turned[0], turned[1]), column[0]),
-            jnp.where(chosen, jnp.where(stays, turned[1], turned[2]), column[1]),
-            jnp.where(chosen, turned[2], column[2]),
+            jnp.where(chosen, jnp.where(stays, rolled[0], rolled[1]), column[0]),
+            jnp.where(chosen, jnp.where(stays, rolled[1], rolled[2]), column[1]),
+            jnp.where(chosen, rolled[2], column[2]),
         ]
     window = jnp.concatenate(column[:2], axis=1).astype(BF16)
-    for move in moves:
-        move.wait()
-    copies = out_ref.shape[0]
+    moves[2].wait()
+    for upper, row in ((0, 0), (1, radii - 1)):
+        for c in range(COMP):
+            for a in range(azimuths):
+                place = c * azimuths + a
+                line_ref[upper, place : place + 1, :] = adj_ref[c, a, row : row + 1, :]
+        line_ref[upper, 10:16, :] = jnp.zeros((6, 128), F32)
+    sends = []
+    for copy in range(copies):
+        upper = jnp.where((copy + FIRST_GROUP) % copies > group, 1, 0)
+        sends.append(
+            pltpu.make_async_copy(line_ref.at[upper], out_hbm.at[copy, pl.ds(count, 16)], sems.at[10 + copy])
+        )
+        sends[-1].start()
+    even = odd == 0
+    inner_ref[...] = jnp.where(even, adj_ref[:, azimuths - 1], adj_ref[:, 0])
+    outer_ref[...] = jnp.where(even, adj_ref[:, 0], adj_ref[:, azimuths - 1])
     for t in range(tiles):
+        if t == 0:
+            moves[3].wait()
+            moves[4].wait()
+        if t == tiles // 2:
+            moves[5].wait()
+            moves[6].wait()
         span = slice(t * TILE, (t + 1) * TILE)
         projected = lax.dot_general(
             window[t * observers : (t + 1) * observers],
@@ -77,22 +120,16 @@
             preferred_element_type=F32,
         )
         for c in range(COMP):
-            total = jnp.sum(amp_ref[c, :, span].astype(F32) * projected, axis=0, keepdims=True)
-            for copy in range(copies):
-                out_ref[copy, c * tiles + t : c * tiles + t + 1, :] = total
-    azimuths, radii = adj_ref.shape[1:3]
-    head_ref[...] = adj_ref[:, 0]
-    tail_ref[...] = adj_ref[:, azimuths - 1]
-    for c in range(COMP):
-        for a in range(azimuths):
-            place = COMP * tiles + c * azimuths + a
-            for copy in range(copies):
-                up = jnp.full((1, 128), (copy + FIRST_GROUP) % copies, jnp.int32) > group
-                out_ref[copy, place : place + 1, :] = jnp.where(
-                    up, adj_ref[c, a, radii - 1 : radii, :], adj_ref[c, a, 0:1, :]
-                )
+            part_ref[c * tiles + t : c * tiles + t + 1, :] = jnp.sum(
+                amp_ref[c, :, span].astype(F32) * projected, axis=0, keepdims=True
+            )
     for copy in range(copies):
-        out_ref[copy, 50:56, :] = jnp.zeros((6, 128), F32)
+        sends.append(
+            pltpu.make_async_copy(part_ref, out_hbm.at[copy, pl.ds(0, count)], sems.at[10 + copies + copy])
+        )
+        sends[-1].start()
+    for move in moves[7:] + sends:
+        move.wait()
 
 
 def order(after_ref, block_ref, cell_ref, same_ref, slot_ref, line_ref):
@@ -149,7 +186,7 @@
     out_ref[:, 0, :] = jnp.concatenate([total[:, :128], rest], axis=1)
 
 
-def stencil(part_ref, next_ref, prev_ref, adj_ref, step_ref, jac_ref, out_ref, source_ref):
+def stencil(part_ref, inner_ref, adj_ref, step_ref, jac_ref, out_ref, source_ref, mix_ref):
     chunks = source_ref.shape[1] // TILE
     source = whole_source(part_ref, COMP * chunks)
     for c in range(COMP):
@@ -164,6 +201,12 @@
     above = jnp.minimum(group + 1, groups - 1)
     has_below = jnp.where(group > 0, 1.0, 0.0)
     has_above = jnp.where(group < groups - 1, 1.0, 0.0)
+    even = lax.axis_index("cells") % 2 == 0
+    half = jnp.where(even, -0.5, 0.5)
+    for k in range(COMP):
+        for c in range(COMP):
+            weight = jac_ref[0, k, 0, c] * half + (SMOOTHING if k == c else 0.0)
+            mix_ref[k * COMP + c : k * COMP + c + 1, :] = jnp.full((1, length), weight, F32)
     uppers = part_ref[(above - FIRST_GROUP + groups) % groups, 40:56, :] * has_above
     lowers = part_ref[(below - FIRST_GROUP + groups) % groups, 40:56, :] * has_below
     for a in range(azimuths):
@@ -171,8 +214,8 @@
         pairs = [[], [], []]
         for c in range(COMP):
             x = centre[c]
-            ahead = next_ref[c] if a == azimuths - 1 else adj_ref[c, a + 1]
-            behind = prev_ref[c] if a == 0 else adj_ref[c, a - 1]
+            ahead = jnp.where(even, inner_ref[c], 0.0) if a == azimuths - 1 else adj_ref[c, a + 1]
+            behind = jnp.where(even, 0.0, inner_ref[c]) if a == 0 else adj_ref[c, a - 1]
             pairs[0].append((ahead, behind))
             place = c * azimuths + a
             upper = uppers[place : place + 1]
@@ -201,44 +244,57 @@
             out_ref[c, a] = centre[c] + step_ref[a] * summed
 
 
-def land(got_ref, base_ref, out_ref):
+def land(got_ref, base_ref, outer_ref, step_ref, mix_ref, source_ref, out_ref, source_hbm, sem):
+    move = pltpu.make_async_copy(source_ref, source_hbm, sem)
+    move.start()
     group = lax.axis_index("obs")
     azimuths, radii, length = base_ref.shape[1:]
     radii_all = radii * lax.axis_size("obs")
-    local_rows = azimuths * radii
     got = jnp.concatenate([got_ref[:, :128].T, got_ref[:, 128:].T], axis=0)
     sources = got_ref.shape[0]
     high = got.astype(BF16).astype(F32)
     low = got - high
     cell = got[COMP * CAP : (COMP + 1) * CAP].astype(jnp.int32)
-    cell_row = cell >> 7
-    cell_lane = cell & 127
-    local = iota((local_rows, sources), 0)
-    wanted = (local // radii) * radii_all + local % radii + group * radii
-    total = jnp.zeros((2 * COMP * local_rows, length), F32)
+    cell_row = (cell // length % radii_all).astype(F32)
+    cell_column = (cell // (length * radii_all) * length + cell % length).astype(F32)
+    wanted = (iota((radii, sources), 0) + group * radii).astype(F32).astype(BF16)
+    columns = azimuths * length
+    column = iota((columns, sources), 0).astype(F32).astype(BF16)
+    one, none = jnp.ones((), BF16), jnp.zeros((), BF16)
+    total = jnp.zeros((2 * COMP * radii, columns), F32)
     for first in range(0, CAP, 2):
-        values, lanes = [], []
-        for k in (first, first + 1):
-            here = jnp.where(wanted == cell_row[k : k + 1], 1.0, 0.0).astype(BF16)
+        values, places = [], []
+        for k in range(first, first + 2):
+            row = jnp.broadcast_to(cell_row[k : k + 1], wanted.shape).astype(BF16)
+            here = jnp.where(wanted == row, one, none)
             values.append(
                 jnp.concatenate(
                     [
-                        jnp.broadcast_to(part[c * CAP + k : c * CAP + k + 1], (local_rows, sources)).astype(BF16) * here
+                        jnp.broadcast_to(part[c * CAP + k : c * CAP + k + 1], wanted.shape).astype(BF16) * here
                         for part in (high, low)
                         for c in range(COMP)
                     ],
                     axis=0,
                 )
             )
-            lanes.append(jnp.where(iota((length, sources), 0) == cell_lane[k : k + 1], 1.0, 0.0).astype(BF16))
+            at = jnp.broadcast_to(cell_column[k : k + 1], column.shape).astype(BF16)
+            places.append(jnp.where(column == at, one, none))
         total = total + lax.dot_general(
-            jnp.concatenate(values, axis=1), jnp.concatenate(lanes, axis=1), NT, preferred_element_type=F32
-        )
-    half = COMP * local_rows
+            jnp.concatenate(values, axis=1), jnp.concatenate(places, axis=1), NT, preferred_element_type=F32
+        )
+    half = COMP * radii
+    edge = jnp.where(lax.axis_index("cells") % 2 == 0, 0, azimuths - 1)
+    steps = [jnp.where(edge == a, step_ref[a], 0.0) for a in range(azimuths)]
     for c in range(COMP):
+        spill = jnp.zeros((radii, length), F32)
+        for k in range(COMP):
+            spill = spill + mix_ref[k * COMP + c : k * COMP + c + 1, :] * outer_ref[k]
         for a in range(azimuths):
-            start = (c * azimuths + a) * radii
-            out_ref[c, a] = base_ref[c, a] + (total[start : start + radii] + total[half + start : half + start + radii])
+            rows = slice(c * radii, (c + 1) * radii)
+            lower = slice(half + c * radii, half + (c + 1) * radii)
+            span = slice(a * length, (a + 1) * length)
+            out_ref[c, a] = base_ref[c, a] + steps[a] * spill + (total[rows, span] + total[lower, span])
+    move.wait()
 
 
 def turned(size, first):
@@ -261,24 +317,35 @@
     amp = amplitude.transpose(1, 0, 2)
     edge = pltpu.VMEM((COMP,) + adjoint.shape[2:], F32)
 
-    partial_copies, head, tail = pl.pallas_call(
+    partial_copies, inner, outer, adjoint_near, blocks_near, cells_near, step_near = pl.pallas_call(
         project,
-        out_shape=(pltpu.VMEM((groups, 56, TILE), F32), edge, edge),
-        in_specs=[VMEM, VMEM, ANY, ANY, ANY],
-        out_specs=(VMEM, VMEM, VMEM),
+        out_shape=(
+            jax.ShapeDtypeStruct((groups, 56, TILE), F32),
+            edge,
+            edge,
+            pltpu.VMEM(adjoint.shape, F32),
+            pltpu.VMEM(blocks2.shape, jnp.int32),
+            pltpu.VMEM(cells2.shape, jnp.int32),
+            pltpu.VMEM(step_size.shape, F32),
+        ),
+        in_specs=[ANY] * 8,
+        out_specs=(ANY,) + (VMEM,) * 6,
         scratch_shapes=[
+            pltpu.VMEM(histories.shape, BF16),
+            pltpu.VMEM((chunks, histories.shape[0]), jnp.int32),
+            pltpu.VMEM(weights.shape, BF16),
             pltpu.VMEM(amp.shape, BF16),
-            pltpu.VMEM(weights.shape, BF16),
-            pltpu.VMEM(adjoint.shape, F32),
-            pltpu.SemaphoreType.DMA((3,)),
+            pltpu.VMEM((COMP * chunks, TILE), F32),
+            pltpu.VMEM((2, 16, TILE), F32),
+            pltpu.SemaphoreType.DMA((10 + 2 * groups,)),
         ],
         name="project",
-    )(histories, retarded.T, amp, weights, adjoint)
+    )(histories, retarded.T, adjoint, weights, amp, blocks2, cells2, step_size)
     parts = lax.all_to_all(
         partial_copies, "obs", 0, 0, axis_index_groups=turned(groups, FIRST_GROUP), tiled=True
     )
-    behind = lax.ppermute(tail, "cells", [(i, (i + 1) % count) for i in range(count)])
-    ahead = lax.ppermute(head, "cells", [((i + 1) % count, i) for i in range(count)])
+    inner = lax.ppermute(inner, "cells", [(i, i ^ 1) for i in range(count)])
+    outer = lax.ppermute(outer, "cells", [(i, ((i + 1 ^ 1) - 1) % count) for i in range(count)])
 
     same, slot, lines = pl.pallas_call(
         order,
@@ -290,7 +357,7 @@
         in_specs=[ANY, VMEM, VMEM],
         out_specs=(VMEM, VMEM, VMEM),
         name="order",
-    )(partial_copies, blocks2, cells2)
+    )(partial_copies, near(blocks_near), near(cells_near))
     outgoing = pl.pallas_call(
         pack,
         out_shape=jax.ShapeDtypeStruct((count, 1, 256), F32),
@@ -302,20 +369,28 @@
         outgoing, "cells", 0, 0, axis_index_groups=turned(count, FIRST_CELL), tiled=True
     )
 
-    base, panel_source = pl.pallas_call(
+    base, source, mix = pl.pallas_call(
         stencil,
-        out_shape=(pltpu.VMEM(adjoint.shape, F32), jax.ShapeDtypeStruct((COMP, panels), F32)),
-        in_specs=[VMEM] * 5 + [SMEM],
-        out_specs=(VMEM, VMEM),
+        out_shape=(
+            pltpu.VMEM(adjoint.shape, F32),
+            pltpu.VMEM((COMP, panels), F32),
+            pltpu.VMEM((32, adjoint.shape[3]), F32),
+        ),
+        in_specs=[VMEM] * 4 + [SMEM],
+        out_specs=(VMEM, VMEM, VMEM),
         name="stencil",
-    )(near(parts), near(ahead), near(behind), adjoint, step_size, jacobian.transpose(1, 2, 0, 3))
-    adjoint_next = pl.pallas_call(
+    )(near(parts), near(inner), near(adjoint_near), near(step_near), jacobian.transpose(1, 2, 0, 3))
+    adjoint_next, panel_source = pl.pallas_call(
         land,
-        out_shape=jax.ShapeDtypeStruct(adjoint.shape, F32),
-        in_specs=[VMEM] * 2,
-        out_specs=VMEM,
+        out_shape=(
+            jax.ShapeDtypeStruct(adjoint.shape, F32),
+            jax.ShapeDtypeStruct((COMP, panels), F32),
+        ),
+        in_specs=[VMEM] * 6,
+        out_specs=(VMEM, ANY),
+        scratch_shapes=[pltpu.SemaphoreType.DMA],
         name="land",
-    )(near(received.reshape(count, 256)), near(base))
+    )(near(received.reshape(count, 256)), near(base), near(outer), near(step_near), near(mix), near(source))
     return adjoint_next, panel_source
 
 

time: 51.3 us -> 45.4 us (0.88)
  the two profiles are of different devices: /device:TPU:8 before, /device:TPU:128 now
where the time goes in v5:
time: 45.4 us; the launch traced here: 45.1 us
  starting transfers between devices  26.9 us (59%)
  waiting for transfers between devices  10.8 us (24%)
  Pallas kernels  6.61 us (15%)
  between operations  0.7 us (2%)
    all_to_all x1, starting transfers between devices, on_device(): lax.all_to_all(outgoing, 'cells', 0, 0, axis_index_groups=turned(count, F...  13.4 us
    all_to_all x1, starting transfers between devices, on_device(): lax.all_to_all(partial_copies, 'obs', 0, 0, axis_index_groups=turned(grou...  9.05 us
    ppermute x1, waiting for transfers between devices, on_device(): lax.ppermute(outer, 'cells', [(i, ((i + 1 ^ 1) - 1) % count) for i in ran...  6.03 us
    all_to_all x1, waiting for transfers between devices, on_device(): lax.all_to_all(partial_copies, 'obs', 0, 0, axis_index_groups=turned(grou...  4.81 us
    pallas_call x1, Pallas kernels, on_device(): pl.pallas_call(project, out_shape=(jax.ShapeDtypeStruct((groups, 56, TILE...  2.63 us
    ppermute x1, starting transfers between devices, on_device(): lax.ppermute(outer, 'cells', [(i, ((i + 1 ^ 1) - 1) % count) for i in ran...  2.45 us
    ppermute x1, starting transfers between devices, on_device(): inner = lax.ppermute(inner, 'cells', [(i, i ^ 1) for i in range(count)])  2.03 us
    pallas_call x1, Pallas kernels, on_device(): pl.pallas_call(land, out_shape=(jax.ShapeDtypeStruct(adjoint.shape, F32),...  1.6 us
  transfers between devices with their start and end apart: 4, of which 2 were waited for; matrix products, arithmetic and copies ran while one was open for 0% of the time, Pallas kernels for 3%

profile of v5, /device:TPU:128, one launch (start us, length us, event | category | flops | bytes accessed | tf_op | source)
XLA Modules:
  0.0 45.1 jit_solution(18316859313085208834)
XLA Ops:
  0.6 2.6 %project.1 = (f32[4,56,128]{2,1,0:T(8,128)}, f32[5,16,128]{2,1,0:T(8,128)S(1)}, f32[5,16,128]{2,1,0:T(8,128)S(1)}, f32[5,2,16,128]{3,2,1,0:T(8,128)S(1)}, s32[8,...) custom-call(bf16[16,384]{1,0:T(8,128)(2,1)} %hist_hbm.1, s32[8,16]{1,0:T(8,128)} %bitcast.11, ...), custom_call_target="tpu_custom_call" | custom-call | tf_op jit(solution)/shard_map/project/pallas_call | solution.py:320
  3.3 9.1 %all-to-all-start = ((f32[4,56,128]{2,1,0:T(8,128)}), f32[4,56,128]{2,1,0:T(8,128)S(1)}, u32[]{:S(2)}, u32[]{:S(2)}) async-start(f32[4,56,128]{2,1,0:T(8,128)} %get-tuple-element.15.after_ref), calls=%async_computation | async-start | bytes 229376 | tf_op jit(solution)/shard_map/all_to_all | solution.py:344
  12.3 0.3 order.1
  12.6 4.8 %all-to-all-done.part_ref = f32[4,56,128]{2,1,0:T(8,128)S(1)} async-done(((f32[4,56,128]{2,1,0:T(8,128)}), f32[4,56,128]{2,1,0:T(8,128)S(1)}, u32[]{:S(2)}, u32[]{:S(2)}) %all-to-all-start) | async-done | bytes 114720 | tf_op jit(solution)/shard_map/all_to_all | solution.py:344
  17.4 1.1 %pack.1 = f32[128,1,256]{2,1,0:T(1,128)} custom-call(f32[4,56,128]{2,1,0:T(8,128)S(1)} %all-to-all-done.part_ref, bf16[8,128,128]{2,1,0:T(8,128)(2,1)S(1)} %get-tuple-element.18.same_ref, bf16[8,32,128]{2,1,0:T(8,128)(2,1)S(1)} %get-tuple-element.19.slot_ref, f32[8,128]{1,0:T(8,128)S(1)} %get-tuple-element.20.line_ref), custom_call_target="tpu_custom_call" | custom-call | tf_op jit(solution)/shard_map/pack/pallas_call | solution.py:361
  18.5 13.4 %all-to-all-start.1 = ((f32[128,1,256]{2,1,0:T(1,128)}), f32[128,1,256]{2,1,0:T(1,128)S(1)}, u32[]{:S(2)}, u32[]{:S(2)}) async-start(f32[128,1,256]{2,1,0:T(1,128)} %pack.1), calls=%async_computation.1 | async-start | bytes 262144 | tf_op jit(solution)/shard_map/all_to_all | solution.py:368
  31.9 2.0 %collective-permute-start = (f32[5,16,128]{2,1,0:T(8,128)S(1)}, f32[5,16,128]{2,1,0:T(8,128)S(1)}, u32[]{:S(2)}, u32[]{:S(2)}) collective-permute-start(f32[5,16,128]{2,1,0:T(8,128)S(1)} %get-tuple-element.21), channel_id=1, source_target_pairs={{0,4},{4,0},{8,12},{12,8},{16,20},{20,16},{24,28},{28,24},{32,36},... | collective-permute-start | bytes 122888 | tf_op jit(solution)/shard_map/ppermute | solution.py:347
  33.9 2.5 %collective-permute-start.1 = (f32[5,16,128]{2,1,0:T(8,128)S(1)}, f32[5,16,128]{2,1,0:T(8,128)S(1)}, u32[]{:S(2)}, u32[]{:S(2)}) collective-permute-start(f32[5,16,128]{2,1,0:T(8,128)S(1)} %get-tuple-element.25), channel_id=1, source_target_pairs={{0,508},{4,8},{8,4},{12,16},{16,12},{20,24},{24,20},{28,32},{32,28... | collective-permute-start | bytes 122888 | tf_op jit(solution)/shard_map/ppermute | solution.py:348
  36.4 0.0 collective-permute-done.inner_ref
  36.4 1.0 %stencil.1 = (f32[5,2,16,128]{3,2,1,0:T(8,128)S(1)}, f32[5,1024]{1,0:T(8,128)S(1)}, f32[32,128]{1,0:T(8,128)S(1)}) custom-call(f32[4,56,128]{2,1,0:T(8,128)S(1)} %all-to-all-done.part_ref, f32[5,16,128]{2,1,0:T(8,128)S(1)} %collective-permute-done.inner_ref, f32[5,2,16,128]{3,2,1,0:T(8,128)S(1)} %get-tuple-element.22.adj_ref, ...), custom_call_target="tpu_custom_call" | custom-call | tf_op jit(solution)/shard_map/stencil/pallas_call | solution.py:372
  37.4 0.0 all-to-all-done.1
  37.4 6.0 %collective-permute-done.1.outer_ref = f32[5,16,128]{2,1,0:T(8,128)S(1)} collective-permute-done((f32[5,16,128]{2,1,0:T(8,128)S(1)}, f32[5,16,128]{2,1,0:T(8,128)S(1)}, u32[]{:S(2)}, u32[]{:S(2)}) %collective-permute-start.1) | collective-permute-done | bytes 40992 | tf_op jit(solution)/shard_map/ppermute | solution.py:348
  43.5 1.6 %land.1 = (f32[5,2,16,128]{3,2,1,0:T(8,128)}, f32[5,1024]{1,0:T(8,128)}) custom-call(f32[128,256]{1,0:T(8,128)S(1)} %bitcast.8, f32[5,2,16,128]{3,2,1,0:T(8,128)S(1)} %get-tuple-element.24.base_ref, f32[5,16,128]{2,1,0:T(8,128)S(1)} %collective-permute-done.1.outer_ref, f32[2,16,128]{2,1,0:T(8,128)S(1)} %get-tuple-element.23.step_ref, ...), custom_call_target="tpu_custom_call" | custom-call | tf_op jit(solution)/shard_map/land/pallas_call | solution.py:383
  (1 shorter events, 0.0 us)
Async XLA Ops:
  3.3 14.2 %all-to-all-start = ((f32[4,56,128]{2,1,0:T(8,128)}), f32[4,56,128]{2,1,0:T(8,128)S(1)}, u32[]{:S(2)}, u32[]{:S(2)}) async-start(f32[4,56,128]{2,1,0:T(8,128)} %get-tuple-element.15.after_ref), calls=%async_computation | async-start | bytes 229376 | tf_op jit(solution)/shard_map/all_to_all | solution.py:344
  18.5 18.9 %all-to-all-start.1 = ((f32[128,1,256]{2,1,0:T(1,128)}), f32[128,1,256]{2,1,0:T(1,128)S(1)}, u32[]{:S(2)}, u32[]{:S(2)}) async-start(f32[128,1,256]{2,1,0:T(1,128)} %pack.1), calls=%async_computation.1 | async-start | bytes 262144 | tf_op jit(solution)/shard_map/all_to_all | solution.py:368
  31.9 4.5 %collective-permute-start = (f32[5,16,128]{2,1,0:T(8,128)S(1)}, f32[5,16,128]{2,1,0:T(8,128)S(1)}, u32[]{:S(2)}, u32[]{:S(2)}) collective-permute-start(f32[5,16,128]{2,1,0:T(8,128)S(1)} %get-tuple-element.21), channel_id=1, source_target_pairs={{0,4},{4,0},{8,12},{12,8},{16,20},{20,16},{24,28},{28,24},{32,36},... | collective-permute-start | bytes 122888 | tf_op jit(solution)/shard_map/ppermute | solution.py:347
  33.9 9.5 %collective-permute-start.1 = (f32[5,16,128]{2,1,0:T(8,128)S(1)}, f32[5,16,128]{2,1,0:T(8,128)S(1)}, u32[]{:S(2)}, u32[]{:S(2)}) collective-permute-start(f32[5,16,128]{2,1,0:T(8,128)S(1)} %get-tuple-element.25), channel_id=1, source_target_pairs={{0,508},{4,8},{8,4},{12,16},{16,12},{20,24},{24,20},{28,32},{32,28... | collective-permute-start | bytes 122888 | tf_op jit(solution)/shard_map/ppermute | solution.py:348

commit v6 on v5

--- a/solution.py
+++ b/solution.py
@@ -13,7 +13,7 @@
 F32 = jnp.float32
 BF16 = jnp.bfloat16
 NT = (((1,), (1,)), ((), ()))
-FIRST_CELL = 75
+FIRST_CELL = 79
 FIRST_GROUP = 2
 
 VMEM = pl.BlockSpec(memory_space=pltpu.MemorySpace.VMEM)
@@ -25,14 +25,31 @@
     return lax.broadcasted_iota(jnp.int32, shape, dim)
 
 
+def order(block_ref, cell_ref, same_ref, slot_ref, line_ref):
+    chunks, width = block_ref.shape
+    blocks = 128
+    mark = jnp.where((iota((width, 2 * width), 0) < iota((width, 2 * width), 1)), 1.0, 0.0).astype(BF16)
+    line_ref[...] = cell_ref[...].astype(F32)
+    named = (iota((blocks, width), 0) + FIRST_CELL) % blocks
+    before = jnp.zeros((blocks, width), F32)
+    for j in range(chunks):
+        same = named == block_ref[j : j + 1, :]
+        marked = jnp.where(same, 1.0, 0.0).astype(BF16)
+        same_ref[j] = marked
+        counted = jnp.dot(marked, mark, preferred_element_type=F32)
+        rank = jnp.sum(jnp.where(same, counted[:, :width] + before, 0.0), axis=0, keepdims=True)
+        slot_ref[j] = jnp.where(iota((CAP, width), 0).astype(F32) == rank, 1.0, 0.0).astype(BF16)
+        before = before + counted[:, width:]
+
+
 def project(
     hist_hbm, ret_hbm, adj_hbm, weight_hbm, amp_hbm, block_hbm, cell_hbm, step_hbm,
-    out_hbm, inner_ref, outer_ref, adj_ref, block_ref, cell_ref, step_ref,
-    hist_ref, ret_ref, weight_ref, amp_ref, part_ref, line_ref, sems,
+    out_ref, inner_ref, outer_ref, adj_ref, step_ref, same_ref, slot_ref, cell_line_ref,
+    hist_ref, ret_ref, weight_ref, amp_ref, block_ref, cell_ref, part_ref, sems,
 ):
     group = lax.axis_index("obs")
     odd = lax.axis_index("cells") % 2
-    copies = out_hbm.shape[0]
+    copies = out_ref.shape[0]
     tiles, observers = ret_hbm.shape
     azimuths, radii = adj_ref.shape[1:3]
     count = COMP * tiles
@@ -89,22 +106,22 @@
         ]
     window = jnp.concatenate(column[:2], axis=1).astype(BF16)
     moves[2].wait()
-    for upper, row in ((0, 0), (1, radii - 1)):
-        for c in range(COMP):
-            for a in range(azimuths):
-                place = c * azimuths + a
-                line_ref[upper, place : place + 1, :] = adj_ref[c, a, row : row + 1, :]
-        line_ref[upper, 10:16, :] = jnp.zeros((6, 128), F32)
-    sends = []
+    for c in range(COMP):
+        for a in range(azimuths):
+            place = count + c * azimuths + a
+            for copy in range(copies):
+                up = jnp.full((1, 128), (copy + FIRST_GROUP) % copies, jnp.int32) > group
+                out_ref[copy, place : place + 1, :] = jnp.where(
+                    up, adj_ref[c, a, radii - 1 : radii, :], adj_ref[c, a, 0:1, :]
+                )
     for copy in range(copies):
-        upper = jnp.where((copy + FIRST_GROUP) % copies > group, 1, 0)
-        sends.append(
-            pltpu.make_async_copy(line_ref.at[upper], out_hbm.at[copy, pl.ds(count, 16)], sems.at[10 + copy])
-        )
-        sends[-1].start()
+        out_ref[copy, count + 10 : count + 16, :] = jnp.zeros((6, 128), F32)
     even = odd == 0
     inner_ref[...] = jnp.where(even, adj_ref[:, azimuths - 1], adj_ref[:, 0])
     outer_ref[...] = jnp.where(even, adj_ref[:, 0], adj_ref[:, azimuths - 1])
+    moves[7].wait()
+    moves[8].wait()
+    order(block_ref, cell_ref, same_ref, slot_ref, cell_line_ref)
     for t in range(tiles):
         if t == 0:
             moves[3].wait()
@@ -124,29 +141,8 @@
                 amp_ref[c, :, span].astype(F32) * projected, axis=0, keepdims=True
             )
     for copy in range(copies):
-        sends.append(
-            pltpu.make_async_copy(part_ref, out_hbm.at[copy, pl.ds(0, count)], sems.at[10 + copies + copy])
-        )
-        sends[-1].start()
-    for move in moves[7:] + sends:
-        move.wait()
-
-
-def order(after_ref, block_ref, cell_ref, same_ref, slot_ref, line_ref):
-    chunks, width = block_ref.shape
-    blocks = 128
-    mark = jnp.where((iota((width, 2 * width), 0) < iota((width, 2 * width), 1)), 1.0, 0.0).astype(BF16)
-    line_ref[...] = cell_ref[...].astype(F32)
-    named = (iota((blocks, width), 0) + FIRST_CELL) % blocks
-    before = jnp.zeros((blocks, width), F32)
-    for j in range(chunks):
-        same = named == block_ref[j : j + 1, :]
-        marked = jnp.where(same, 1.0, 0.0).astype(BF16)
-        same_ref[j] = marked
-        counted = jnp.dot(marked, mark, preferred_element_type=F32)
-        rank = jnp.sum(jnp.where(same, counted[:, :width] + before, 0.0), axis=0, keepdims=True)
-        slot_ref[j] = jnp.where(iota((CAP, width), 0).astype(F32) == rank, 1.0, 0.0).astype(BF16)
-        before = before + counted[:, width:]
+        out_ref[copy, :count, :] = part_ref[...]
+    moves[9].wait()
 
 
 def whole_source(part_ref, count):
@@ -186,7 +182,7 @@
     out_ref[:, 0, :] = jnp.concatenate([total[:, :128], rest], axis=1)
 
 
-def stencil(part_ref, inner_ref, adj_ref, step_ref, jac_ref, out_ref, source_ref, mix_ref):
+def stencil(part_ref, adj_ref, step_ref, jac_ref, out_ref, source_ref, mix_ref):
     chunks = source_ref.shape[1] // TILE
     source = whole_source(part_ref, COMP * chunks)
     for c in range(COMP):
@@ -201,12 +197,10 @@
     above = jnp.minimum(group + 1, groups - 1)
     has_below = jnp.where(group > 0, 1.0, 0.0)
     has_above = jnp.where(group < groups - 1, 1.0, 0.0)
-    even = lax.axis_index("cells") % 2 == 0
-    half = jnp.where(even, -0.5, 0.5)
     for k in range(COMP):
         for c in range(COMP):
-            weight = jac_ref[0, k, 0, c] * half + (SMOOTHING if k == c else 0.0)
-            mix_ref[k * COMP + c : k * COMP + c + 1, :] = jnp.full((1, length), weight, F32)
+            mix_ref[k * COMP + c : k * COMP + c + 1, :] = jnp.full((1, length), 0.5 * jac_ref[0, k, 0, c], F32)
+    none = jnp.zeros((radii, length), F32)
     uppers = part_ref[(above - FIRST_GROUP + groups) % groups, 40:56, :] * has_above
     lowers = part_ref[(below - FIRST_GROUP + groups) % groups, 40:56, :] * has_below
     for a in range(azimuths):
@@ -214,8 +208,8 @@
         pairs = [[], [], []]
         for c in range(COMP):
             x = centre[c]
-            ahead = jnp.where(even, inner_ref[c], 0.0) if a == azimuths - 1 else adj_ref[c, a + 1]
-            behind = jnp.where(even, 0.0, inner_ref[c]) if a == 0 else adj_ref[c, a - 1]
+            ahead = none if a == azimuths - 1 else adj_ref[c, a + 1]
+            behind = none if a == 0 else adj_ref[c, a - 1]
             pairs[0].append((ahead, behind))
             place = c * azimuths + a
             upper = uppers[place : place + 1]
@@ -244,7 +238,7 @@
             out_ref[c, a] = centre[c] + step_ref[a] * summed
 
 
-def land(got_ref, base_ref, outer_ref, step_ref, mix_ref, source_ref, out_ref, source_hbm, sem):
+def land(got_ref, base_ref, inner_ref, outer_ref, step_ref, mix_ref, source_ref, out_ref, source_hbm, sem):
     move = pltpu.make_async_copy(source_ref, source_hbm, sem)
     move.start()
     group = lax.axis_index("obs")
@@ -283,17 +277,19 @@
             jnp.concatenate(values, axis=1), jnp.concatenate(places, axis=1), NT, preferred_element_type=F32
         )
     half = COMP * radii
-    edge = jnp.where(lax.axis_index("cells") % 2 == 0, 0, azimuths - 1)
-    steps = [jnp.where(edge == a, step_ref[a], 0.0) for a in range(azimuths)]
+    even = lax.axis_index("cells") % 2 == 0
+    behind = jnp.where(even, outer_ref[...], inner_ref[...])
+    ahead = jnp.where(even, inner_ref[...], outer_ref[...])
     for c in range(COMP):
-        spill = jnp.zeros((radii, length), F32)
-        for k in range(COMP):
-            spill = spill + mix_ref[k * COMP + c : k * COMP + c + 1, :] * outer_ref[k]
+        mix = [mix_ref[k * COMP + c : k * COMP + c + 1, :] for k in range(COMP)]
+        spills = [jnp.zeros((radii, length), F32)] * azimuths
+        spills[0] = spills[0] + SMOOTHING * behind[c] - sum(mix[k] * behind[k] for k in range(COMP))
+        spills[-1] = spills[-1] + SMOOTHING * ahead[c] + sum(mix[k] * ahead[k] for k in range(COMP))
         for a in range(azimuths):
             rows = slice(c * radii, (c + 1) * radii)
             lower = slice(half + c * radii, half + (c + 1) * radii)
             span = slice(a * length, (a + 1) * length)
-            out_ref[c, a] = base_ref[c, a] + steps[a] * spill + (total[rows, span] + total[lower, span])
+            out_ref[c, a] = base_ref[c, a] + step_ref[a] * spills[a] + (total[rows, span] + total[lower, span])
     move.wait()
 
 
@@ -317,27 +313,29 @@
     amp = amplitude.transpose(1, 0, 2)
     edge = pltpu.VMEM((COMP,) + adjoint.shape[2:], F32)
 
-    partial_copies, inner, outer, adjoint_near, blocks_near, cells_near, step_near = pl.pallas_call(
+    partial_copies, inner, outer, adjoint_near, step_near, same, slot, lines = pl.pallas_call(
         project,
         out_shape=(
-            jax.ShapeDtypeStruct((groups, 56, TILE), F32),
+            pltpu.VMEM((groups, 56, TILE), F32),
             edge,
             edge,
             pltpu.VMEM(adjoint.shape, F32),
-            pltpu.VMEM(blocks2.shape, jnp.int32),
-            pltpu.VMEM(cells2.shape, jnp.int32),
             pltpu.VMEM(step_size.shape, F32),
+            pltpu.VMEM((chunks, 128, TILE), BF16),
+            pltpu.VMEM((chunks, CAP, TILE), BF16),
+            pltpu.VMEM((chunks, TILE), F32),
         ),
         in_specs=[ANY] * 8,
-        out_specs=(ANY,) + (VMEM,) * 6,
+        out_specs=(VMEM,) * 8,
         scratch_shapes=[
             pltpu.VMEM(histories.shape, BF16),
             pltpu.VMEM((chunks, histories.shape[0]), jnp.int32),
             pltpu.VMEM(weights.shape, BF16),
             pltpu.VMEM(amp.shape, BF16),
+            pltpu.VMEM(blocks2.shape, jnp.int32),
+            pltpu.VMEM(cells2.shape, jnp.int32),
             pltpu.VMEM((COMP * chunks, TILE), F32),
-            pltpu.VMEM((2, 16, TILE), F32),
-            pltpu.SemaphoreType.DMA((10 + 2 * groups,)),
+            pltpu.SemaphoreType.DMA((10,)),
         ],
         name="project",
     )(histories, retarded.T, adjoint, weights, amp, blocks2, cells2, step_size)
@@ -347,17 +345,6 @@
     inner = lax.ppermute(inner, "cells", [(i, i ^ 1) for i in range(count)])
     outer = lax.ppermute(outer, "cells", [(i, ((i + 1 ^ 1) - 1) % count) for i in range(count)])
 
-    same, slot, lines = pl.pallas_call(
-        order,
-        out_shape=(
-            pltpu.VMEM((chunks, 128, TILE), BF16),
-            pltpu.VMEM((chunks, CAP, TILE), BF16),
-            pltpu.VMEM((chunks, TILE), F32),
-        ),
-        in_specs=[ANY, VMEM, VMEM],
-        out_specs=(VMEM, VMEM, VMEM),
-        name="order",
-    )(partial_copies, near(blocks_near), near(cells_near))
     outgoing = pl.pallas_call(
         pack,
         out_shape=jax.ShapeDtypeStruct((count, 1, 256), F32),
@@ -376,21 +363,21 @@
             pltpu.VMEM((COMP, panels), F32),
             pltpu.VMEM((32, adjoint.shape[3]), F32),
         ),
-        in_specs=[VMEM] * 4 + [SMEM],
+        in_specs=[VMEM] * 3 + [SMEM],
         out_specs=(VMEM, VMEM, VMEM),
         name="stencil",
-    )(near(parts), near(inner), near(adjoint_near), near(step_near), jacobian.transpose(1, 2, 0, 3))
+    )(near(parts), near(adjoint_near), near(step_near), jacobian.transpose(1, 2, 0, 3))
     adjoint_next, panel_source = pl.pallas_call(
         land,
         out_shape=(
             jax.ShapeDtypeStruct(adjoint.shape, F32),
             jax.ShapeDtypeStruct((COMP, panels), F32),
         ),
-        in_specs=[VMEM] * 6,
+        in_specs=[VMEM] * 7,
         out_specs=(VMEM, ANY),
         scratch_shapes=[pltpu.SemaphoreType.DMA],
         name="land",
-    )(near(received.reshape(count, 256)), near(base), near(outer), near(step_near), near(mix), near(source))
+    )(near(received.reshape(count, 256)), near(base), near(inner), near(outer), near(step_near), near(mix), near(source))
     return adjoint_next, panel_source
 
 

time: 45.4 us -> 44.7 us (0.985)
  blocking collectives: 0 us -> 14 us
  starting transfers between devices: 26.9 us -> 17.8 us
  waiting for transfers between devices: 10.8 us -> 6.08 us
  Pallas kernels: 6.61 us -> 5.85 us
    all_to_all x0 -> x1, blocking collectives: none -> 14 us  [on_device(): lax.all_to_all(partial_copies, 'obs', 0, 0, axis_index_groups=turned(grou...]
    all_to_all x1 -> x0, starting transfers between devices: 9.05 us -> none  [on_device(): lax.all_to_all(partial_copies, 'obs', 0, 0, axis_index_groups=turned(grou...]
    all_to_all x1 -> x0, waiting for transfers between devices: 4.81 us -> none  [on_device(): lax.all_to_all(partial_copies, 'obs', 0, 0, axis_index_groups=turned(grou...]
    pallas_call x2 -> x1, Pallas kernels: 2.94 us -> 2.24 us  [on_device(): pl.pallas_call(project, out_shape=(pltpu.VMEM((groups, 56, TILE), F32), e...]
  transfers between devices with their start and end apart: 4 -> 3, of which waited for: 2 -> 1; matrix products, arithmetic and copies ran while one was open for 0% -> 0% of each run, Pallas kernels for 3% -> 2%
where the time goes in v6:
time: 44.7 us; the launch traced here: 44.4 us
  starting transfers between devices  17.8 us (40%)
  blocking collectives  14 us (31%)
  waiting for transfers between devices  6.08 us (14%)
  Pallas kernels  5.85 us (13%)
  between operations  0.7 us (2%)
    all_to_all x1, blocking collectives, on_device(): lax.all_to_all(partial_copies, 'obs', 0, 0, axis_index_groups=turned(grou...  14 us
    all_to_all x1, starting transfers between devices, on_device(): lax.all_to_all(outgoing, 'cells', 0, 0, axis_index_groups=turned(count, F...  13.3 us
    ppermute x1, waiting for transfers between devices, on_device(): lax.ppermute(outer, 'cells', [(i, ((i + 1 ^ 1) - 1) % count) for i in ran...  6.08 us
    ppermute x1, starting transfers between devices, on_device(): lax.ppermute(outer, 'cells', [(i, ((i + 1 ^ 1) - 1) % count) for i in ran...  2.45 us
    pallas_call x1, Pallas kernels, on_device(): pl.pallas_call(project, out_shape=(pltpu.VMEM((groups, 56, TILE), F32), e...  2.24 us
    ppermute x1, starting transfers between devices, on_device(): inner = lax.ppermute(inner, 'cells', [(i, i ^ 1) for i in range(count)])  2.03 us
    pallas_call x1, Pallas kernels, on_device(): pl.pallas_call(land, out_shape=(jax.ShapeDtypeStruct(adjoint.shape, F32),...  1.6 us
    pallas_call x1, Pallas kernels, on_device(): pl.pallas_call(pack, out_shape=jax.ShapeDtypeStruct((count, 1, 256), F32)...  1.05 us
  transfers between devices with their start and end apart: 3, of which 1 were waited for; matrix products, arithmetic and copies ran while one was open for 0% of the time, Pallas kernels for 2%

profile of v6, /device:TPU:128, one launch (start us, length us, event | category | flops | bytes accessed | tf_op | source)
XLA Modules:
  0.0 44.4 jit_solution(15552786240743420841)
XLA Ops:
  0.6 2.2 %project.1 = (f32[4,56,128]{2,1,0:T(8,128)S(1)}, f32[5,16,128]{2,1,0:T(8,128)S(1)}, f32[5,16,128]{2,1,0:T(8,128)S(1)}, f32[5,2,16,128]{3,2,1,0:T(8,128)S(1)}, f3...) custom-call(bf16[16,384]{1,0:T(8,128)(2,1)} %hist_hbm.1, ...), custom_call_target="tpu_custom_call" | custom-call | tf_op jit(solution)/shard_map/project/pallas_call | solution.py:316
  2.9 14.0 %all_to_all.10.part_ref = f32[4,56,128]{2,1,0:T(8,128)S(1)} all-to-all(f32[4,56,128]{2,1,0:T(8,128)S(1)} %get-tuple-element.13), channel_id=1, replica_groups={{2,3,0,1},{6,7,4,5},{10,11,8,9},{14,15,12,13},{18,19,16,17},{22,23,20,2..., dimensions={0} | all-to-all | bytes 229376 | tf_op jit(solution)/shard_map/all_to_all | solution.py:342
  16.8 1.1 %pack.1 = f32[128,1,256]{2,1,0:T(1,128)} custom-call(f32[4,56,128]{2,1,0:T(8,128)S(1)} %all_to_all.10.part_ref, bf16[8,128,128]{2,1,0:T(8,128)(2,1)S(1)} %get-tuple-element.14.same_ref, bf16[8,32,128]{2,1,0:T(8,128)(2,1)S(1)} %get-tuple-element.15.slot_ref, f32[8,128]{1,0:T(8,128)S(1)} %get-tuple-element.16.line_ref), custom_call_target="tpu_custom_call" | custom-call | tf_op jit(solution)/shard_map/pack/pallas_call | solution.py:348
  17.9 13.3 %all-to-all-start.1 = ((f32[128,1,256]{2,1,0:T(1,128)}), f32[128,1,256]{2,1,0:T(1,128)S(1)}, u32[]{:S(2)}, u32[]{:S(2)}) async-start(f32[128,1,256]{2,1,0:T(1,128)} %pack.1), calls=%async_computation.1 | async-start | bytes 262144 | tf_op jit(solution)/shard_map/all_to_all | solution.py:355
  31.2 2.0 %collective-permute-start = (f32[5,16,128]{2,1,0:T(8,128)S(1)}, f32[5,16,128]{2,1,0:T(8,128)S(1)}, u32[]{:S(2)}, u32[]{:S(2)}) collective-permute-start(f32[5,16,128]{2,1,0:T(8,128)S(1)} %get-tuple-element.20), channel_id=1, source_target_pairs={{0,4},{4,0},{8,12},{12,8},{16,20},{20,16},{24,28},{28,24},{32,36},... | collective-permute-start | bytes 122888 | tf_op jit(solution)/shard_map/ppermute | solution.py:345
  33.2 2.5 %collective-permute-start.1 = (f32[5,16,128]{2,1,0:T(8,128)S(1)}, f32[5,16,128]{2,1,0:T(8,128)S(1)}, u32[]{:S(2)}, u32[]{:S(2)}) collective-permute-start(f32[5,16,128]{2,1,0:T(8,128)S(1)} %get-tuple-element.21), channel_id=1, source_target_pairs={{0,508},{4,8},{8,4},{12,16},{16,12},{20,24},{24,20},{28,32},{32,28... | collective-permute-start | bytes 122888 | tf_op jit(solution)/shard_map/ppermute | solution.py:346
  35.7 1.0 %stencil.1 = (f32[5,2,16,128]{3,2,1,0:T(8,128)S(1)}, f32[5,1024]{1,0:T(8,128)S(1)}, f32[32,128]{1,0:T(8,128)S(1)}) custom-call(f32[4,56,128]{2,1,0:T(8,128)S(1)} %all_to_all.10.part_ref, f32[5,2,16,128]{3,2,1,0:T(8,128)S(1)} %get-tuple-element.17.adj_ref, f32[2,16,128]{2,1,0:T(8,128)S(1)} %get-tuple-element.18.step_ref, f32[3,5,1,5]{3,2,1,0:T(1,128)} %bitcast.10), custom_call_target="tpu_custom_call" | custom-call | tf_op jit(solution)/shard_map/stencil/pallas_call | solution.py:359
  36.6 0.0 all-to-all-done.1
  36.7 0.0 collective-permute-done.inner_ref
  36.7 6.1 %collective-permute-done.1.outer_ref = f32[5,16,128]{2,1,0:T(8,128)S(1)} collective-permute-done((f32[5,16,128]{2,1,0:T(8,128)S(1)}, f32[5,16,128]{2,1,0:T(8,128)S(1)}, u32[]{:S(2)}, u32[]{:S(2)}) %collective-permute-start.1) | collective-permute-done | bytes 40992 | tf_op jit(solution)/shard_map/ppermute | solution.py:346
  42.8 1.6 %land.1 = (f32[5,2,16,128]{3,2,1,0:T(8,128)}, f32[5,1024]{1,0:T(8,128)}) custom-call(f32[128,256]{1,0:T(8,128)S(1)} %bitcast.8, f32[5,2,16,128]{3,2,1,0:T(8,128)S(1)} %get-tuple-element.19.base_ref, f32[5,16,128]{2,1,0:T(8,128)S(1)} %collective-permute-done.inner_ref, f32[5,16,128]{2,1,0:T(8,128)S(1)} %collective-permute-done.1.outer_ref, ...), custom_call_target="tpu_custom_call" | custom-call | tf_op jit(solution)/shard_map/land/pallas_call | solution.py:370
  (1 shorter events, 0.0 us)
Async XLA Ops:
  17.9 18.7 %all-to-all-start.1 = ((f32[128,1,256]{2,1,0:T(1,128)}), f32[128,1,256]{2,1,0:T(1,128)S(1)}, u32[]{:S(2)}, u32[]{:S(2)}) async-start(f32[128,1,256]{2,1,0:T(1,128)} %pack.1), calls=%async_computation.1 | async-start | bytes 262144 | tf_op jit(solution)/shard_map/all_to_all | solution.py:355
  31.2 5.5 %collective-permute-start = (f32[5,16,128]{2,1,0:T(8,128)S(1)}, f32[5,16,128]{2,1,0:T(8,128)S(1)}, u32[]{:S(2)}, u32[]{:S(2)}) collective-permute-start(f32[5,16,128]{2,1,0:T(8,128)S(1)} %get-tuple-element.20), channel_id=1, source_target_pairs={{0,4},{4,0},{8,12},{12,8},{16,20},{20,16},{24,28},{28,24},{32,36},... | collective-permute-start | bytes 122888 | tf_op jit(solution)/shard_map/ppermute | solution.py:345
  33.2 9.5 %collective-permute-start.1 = (f32[5,16,128]{2,1,0:T(8,128)S(1)}, f32[5,16,128]{2,1,0:T(8,128)S(1)}, u32[]{:S(2)}, u32[]{:S(2)}) collective-permute-start(f32[5,16,128]{2,1,0:T(8,128)S(1)} %get-tuple-element.21), channel_id=1, source_target_pairs={{0,508},{4,8},{8,4},{12,16},{16,12},{20,24},{24,20},{28,32},{32,28... | collective-permute-start | bytes 122888 | tf_op jit(solution)/shard_map/ppermute | solution.py:346
